TPU v7x, 16 devices: a whole 2x2x2 slice. The times are simulated.
16 devices in a mesh: col: 4 (over z, y), row: 4 (over x, core).
Axes of the slice: x: 2, y: 2, z: 2, core: 2. Of those that a mesh axis runs over, the one named last changes fastest.
Arguments:
- t_amps: float32 [256, 20736], P('row', 'col')
- denoms: float32 [256, 20736], P('row', 'col')
- v_oovv: bfloat16 [256, 20736], P('row', 'col')
- v_vvvv: bfloat16 [20736, 20736], P('row', 'col')
- v_oooo: bfloat16 [256, 256], replicated
- w_direct: bfloat16 [2304, 2304], P(None, 'col')
- w_exch: bfloat16 [2304, 2304], P(None, 'col')
Outputs:
- output: float32 [256, 20736], P('row', 'col')
All inputs are finite; a program needn't handle non-finite values.
Results may differ from a plain program's by a relative error of at most 0.001.
Values are sent between devices in bfloat16 or wider.
A program may use at most 1 GiB of HBM per device.

v0:
```python
import math
import jax
import jax.numpy as jnp
from jax import lax
from jax.sharding import PartitionSpec as P


def solution(mesh):
    n_row = mesh.shape["row"]
    n_col = mesh.shape["col"]
    amp_spec = P("row", "col")
    wide_spec = P(None, "col")

    def local_sweep(t_blk, d_blk, oovv_blk, vvvv_blk, oooo_full, wd_blk, wx_blk):
        rows_dev, cols_dev = t_blk.shape
        n_occ = math.isqrt(oooo_full.shape[0])
        n_virt = wd_blk.shape[0] // n_occ
        occ_row = n_occ // n_row
        occ_col = n_occ // n_col
        t_half = t_blk.astype(jnp.bfloat16)
        t_rows = lax.all_gather(t_half, "col", axis=1, tiled=True)
        t_ladder = lax.all_to_all(t_rows, "row", 1, 0, tiled=True)
        ladder_part = jnp.dot(t_ladder, vvvv_blk, preferred_element_type=jnp.float32)
        t_cols = lax.all_gather(t_half, "row", axis=0, tiled=True)
        x_part = lax.dot_general(oovv_blk, t_cols, (((1,), (1,)), ((), ())), preferred_element_type=jnp.float32)
        x_rows = lax.psum(x_part, "col")
        row_idx = lax.axis_index("row")
        oooo_rows = lax.dynamic_slice_in_dim(oooo_full, row_idx * rows_dev, rows_dev, axis=0)
        hole_mat = (oooo_rows.astype(jnp.float32) + 0.5 * x_rows).astype(jnp.bfloat16)
        hole_part = lax.dot_general(hole_mat, t_half, (((0,), (0,)), ((), ())), preferred_element_type=jnp.float32)
        ladder_sum = lax.psum_scatter(ladder_part + hole_part, "row", scatter_dimension=0, tiled=True)
        t_four = t_rows.reshape(occ_row, n_occ, n_virt, n_virt)
        direct_term = jnp.einsum("ikac,kcjb->ijab", t_four, wd_blk.reshape(n_occ, n_virt, occ_col, n_virt), preferred_element_type=jnp.float32)
        exch_term = jnp.einsum("ikcb,kcja->ijab", t_four, wx_blk.reshape(n_occ, n_virt, occ_col, n_virt), preferred_element_type=jnp.float32)
        ph_back = lax.all_to_all(direct_term - exch_term, "col", 2, 1, tiled=True)
        swap_row = lax.all_to_all(ph_back, "row", 1, 0, tiled=True)
        swap_both = lax.all_to_all(swap_row, "col", 3, 2, tiled=True)
        ph_sym = (ph_back + swap_both.transpose(1, 0, 3, 2)).reshape(rows_dev, cols_dev)
        residual = oovv_blk.astype(jnp.float32) + ladder_sum + ph_sym
        return residual / d_blk

    return jax.shard_map(local_sweep, mesh=mesh, in_specs=(amp_spec, amp_spec, amp_spec, amp_spec, P(), wide_spec, wide_spec), out_specs=amp_spec, check_vma=False)
```

profile of v0, /device:TPU:0, one launch (start us, length us, event | category | flops | bytes accessed | tf_op | source)
XLA Modules:
  0.0 330.7 jit_solution(5112651799233271296)
XLA Ops:
  6.5 2.3 convert_bitcast_fusion
  9.0 1.0 convert_element_type.13
  10.0 38.0 %all-gather.6.cloned.1.call-done = bf16[4,5184,64]{1,2,0:T(8,128)(2,1)} async-done(((bf16[1,5184,64]{1,2,0:T(8,128)(2,1)}), bf16[4,5184,64]{1,2,0:T(8,128)(2,1)}) %all-gather.6.cloned.1.call-update) | async-done | bytes 2654224 | tf_op jit(solution)/shard_map/all_gather | solution.py:21
  48.0 5.3 %copy.48 = bf16[4,5184,64]{1,0,2:T(4,128)(2,1)} copy(bf16[4,5184,64]{1,2,0:T(8,128)(2,1)} %all-gather.6.cloned.1.call-done) | data formatting | bytes 5308416 | tf_op jit(solution)/shard_map/all_gather | solution.py:21
  53.4 4.0 %reshape.20 = bf16[20736,64]{0,1:T(8,128)(2,1)S(1)} reshape(bf16[4,5184,64]{1,0,2:T(4,128)(2,1)} %copy.48) | data formatting | bytes 5308416
  57.3 4.3 %all_to_all.53 = bf16[64,4,5184]{2,1,0:T(4,128)(2,1)} reshape(bf16[64,20736]{1,0:T(8,128)(2,1)S(1)} %bitcast.52) | data formatting | bytes 5308416 | tf_op jit(solution)/shard_map/all_to_all | solution.py:22
  61.6 3.6 %copy.49 = bf16[64,4,5184]{2,0,1:T(8,128)(2,1)} copy(bf16[64,4,5184]{2,1,0:T(4,128)(2,1)} %all_to_all.53) | data formatting | bytes 5308416 | tf_op jit(solution)/shard_map/all_to_all | solution.py:22
  65.2 4.7 %all-to-all-start = ((bf16[64,4,5184]{2,0,1:T(8,128)(2,1)}), bf16[64,4,5184]{2,0,1:T(8,128)(2,1)}, u32[]{:S(2)}, u32[]{:S(2)}) async-start(bf16[64,4,5184]{2,0,1:T(8,128)(2,1)} %copy.49), calls=%async_computation | async-start | bytes 5373952 | tf_op jit(solution)/shard_map/all_to_all | solution.py:22
  70.0 3.3 %all-gather.4.cloned.1.call-done = bf16[256,5184]{1,0:T(8,128)(2,1)} async-done(((bf16[64,5184]{1,0:T(8,128)(2,1)}), bf16[256,5184]{1,0:T(8,128)(2,1)}) %all-gather.4.cloned.1.call-update) | async-done | bytes 2654224 | tf_op jit(solution)/shard_map/all_gather | solution.py:24
  73.3 3.3 %fusion.11 = f32[64,256]{1,0:T(8,128)} fusion(bf16[64,5184]{1,0:T(8,128)(2,1)S(1)} %copy-done.3, bf16[256,5184]{1,0:T(8,128)(2,1)} %all-gather.4.cloned.1.call-done), kind=kOutput, calls=%fused_computation.15 | convolution fusion | flops 169869312 | bytes 3383296 | tf_op jit(solution)/shard_map/dot_general | solution.py:25
  76.9 24.8 %all-to-all-done = bf16[64,4,5184]{2,0,1:T(8,128)(2,1)} async-done(((bf16[64,4,5184]{2,0,1:T(8,128)(2,1)}), bf16[64,4,5184]{2,0,1:T(8,128)(2,1)}, u32[]{:S(2)}, u32[]{:S(2)}) %all-to-all-start) | async-done | bytes 2654240 | tf_op jit(solution)/shard_map/all_to_all | solution.py:22
  101.6 25.9 %fusion.10 = f32[256,5184]{1,0:T(8,128)} fusion(bf16[256,5184]{1,0:T(8,128)(2,1)} %bitcast.4, bf16[5184,5184]{1,0:T(8,128)(2,1)} %param.10), kind=kOutput, calls=%fused_computation.14 | convolution fusion | flops 13759414272 | bytes 61710336 | tf_op jit(solution)/shard_map/dot_general | solution.py:23
  127.5 5.8 %convolution_add_fusion = f32[256,5184]{1,0:T(8,128)} fusion(f32[256,5184]{1,0:T(8,128)} %fusion.10, bf16[64,5184]{1,0:T(8,128)(2,1)S(1)} %copy-done, f32[64,256]{1,0:T(8,128)} %all-reduce.2.cloned.1.call-done, bf16[256,256]{1,0:T(8,128)(2,1)} %param.11, s32[]{:T(128)S(6)} %select_n.3), kind=kOutput, calls=%fused_computation | convolution fusion | flops 171261952 | bytes 11444228 | tf_op jit(solution)/shard_map/dot_general | solution.py:30
  133.4 9.7 %reshape.17 = bf16[16,144,4,144]{1,0,3,2:T(8,128)(2,1)} reshape(bf16[2304,576]{0,1:T(8,128)(2,1)} %param.13) | data formatting | bytes 5308416 | tf_op jit(solution)/shard_map/reshape | solution.py:34
  143.1 9.7 %reshape.15 = bf16[16,144,4,144]{1,0,3,2:T(8,128)(2,1)} reshape(bf16[2304,576]{0,1:T(8,128)(2,1)} %param.12) | data formatting | bytes 5308416 | tf_op jit(solution)/shard_map/reshape | solution.py:33
  152.7 9.3 %reshape.22 = bf16[4,16,144,144,1]{3,2,1,0,4:T(8,128)(2,1)} reshape(bf16[64,20736]{1,0:T(8,128)(2,1)S(1)} %bitcast.53) | data formatting | bytes 5308416 | tf_op jit(solution)/shard_map/reshape | solution.py:32
  162.1 9.7 %fusion = f32[4,144,4,144,1]{1,3,4,2,0:T(8,128)S(1)} fusion(bf16[4,16,144,144,1]{3,2,1,0,4:T(8,128)(2,1)} %reshape.22, bf16[16,144,4,144,1]{1,0,3,2,4:T(8,128)(2,1)} %bitcast.64), kind=kOutput, calls=%fused_computation.2 | convolution fusion | flops 1528823808 | bytes 6635520 | tf_op jit(solution)/shard_map/ikcb,kcja->ijab/dot_general | solution.py:34
  171.8 7.1 %bitcast_subtract_fusion = f32[4,4,144,144]{2,3,0,1:T(8,128)} fusion(f32[4,144,4,144,1]{1,3,4,2,0:T(8,128)S(1)} %fusion, bf16[4,16,144,144,1]{3,2,1,0,4:T(8,128)(2,1)S(1)} %copy-done.2, bf16[16,144,4,144,1]{1,0,3,2,4:T(8,128)(2,1)S(1)} %bitcast.63), kind=kOutput, calls=%fused_computation.6 | convolution fusion | flops 1529155584 | bytes 7962624 | tf_op jit(solution)/shard_map/ikac,kcjb->ijab/dot_general | solution.py:33
  178.9 3.3 %copy.53 = f32[4,4,144,144]{3,0,1,2:T(4,128)S(1)} copy(f32[4,4,144,144]{2,3,0,1:T(8,128)} %bitcast_subtract_fusion) | data formatting | bytes 2654208 | tf_op jit(solution)/shard_map/sub | solution.py:35
  182.2 30.8 %all_to_all.73 = f32[4,4,144,144]{3,0,1,2:T(4,128)S(1)} all-to-all(f32[4,4,144,144]{3,0,1,2:T(4,128)S(1)} %copy.53), channel_id=1, replica_groups=mesh['col'=4,'row'=4] {'col'}, dimensions={2} | all-to-all | bytes 2654208 | tf_op jit(solution)/shard_map/all_to_all | solution.py:35
  213.6 31.0 %all_to_all.74 = f32[4,16,36,144]{3,0,2,1:T(4,128)S(1)} all-to-all(f32[4,16,36,144]{3,0,2,1:T(4,128)S(1)} %bitcast.54), channel_id=1, replica_groups=mesh['col'=4,'row'=4] {'row'}, dimensions={1} | all-to-all | bytes 2654208 | tf_op jit(solution)/shard_map/all_to_all | solution.py:36
  244.5 2.9 copy.56
  247.5 7.9 %copy.57 = f32[16,4,36,144]{2,0,1,3:T(8,128)} copy(f32[16,4,36,144]{3,1,2,0:T(4,128)} %bitcast.58) | data formatting | bytes 2654208 | tf_op jit(solution)/shard_map/all_to_all | solution.py:36
  255.4 7.6 %reshape.27 = f32[4,1,82944]{2,1,0:T(1,128)} reshape(f32[144,4,16,36]{3,2,1,0:T(8,128)} %bitcast.55) | data formatting | bytes 2654208
  263.0 21.8 %all_to_all.75 = f32[4,1,82944]{2,1,0:T(1,128)} all-to-all(f32[4,1,82944]{2,1,0:T(1,128)} %reshape.27), channel_id=1, replica_groups=mesh['col'=4,'row'=4] {'col'}, dimensions={0} | all-to-all | bytes 2654208 | tf_op jit(solution)/shard_map/all_to_all | solution.py:37
  285.3 6.5 %reduce = f32[4,82944]{1,0:T(4,128)} reduce(f32[4,1,82944]{2,1,0:T(1,128)} %all_to_all.75, f32[]{:T(128)} %broadcast), dimensions={1}, to_apply=%all_to_all.65.reduce_sub_computation | reduce | bytes 2654212 | tf_op jit(solution)/shard_map/all_to_all | solution.py:37
  291.8 9.8 %reshape.28 = f32[144,4,16,36]{3,2,1,0:T(8,128)} reshape(f32[4,82944]{1,0:T(4,128)} %reduce) | data formatting | bytes 2654208
  301.5 7.5 %copy.82 = f32[16,4,36,4,36]{2,3,0,4,1:T(4,128)} copy(f32[16,4,36,4,36]{2,0,1,4,3:T(8,128)} %bitcast.56) | data formatting | bytes 2654208 | tf_op jit(solution)/shard_map/all_to_all | solution.py:37
  309.1 5.4 %all_to_all.68 = f32[16,4,144,36]{2,0,3,1:T(8,128)} reshape(f32[16,4,4,36,36]{3,2,0,4,1:T(4,128)} %bitcast.57) | data formatting | bytes 2654208 | tf_op jit(solution)/shard_map/all_to_all | solution.py:37
  314.5 3.5 %bitcast_add_fusion = f32[4,16,36,144]{3,0,2,1:T(4,128)S(1)} fusion(f32[16,4,144,36]{2,0,3,1:T(8,128)} %all_to_all.68, f32[4,4,4,36,144]{4,0,3,2,1:T(4,128)S(1)} %copy.55), kind=kLoop, calls=%fused_computation.7 | loop fusion | flops 331776 | bytes 3981312 | tf_op jit(solution)/shard_map/add | solution.py:38
  318.5 2.1 reshape.18
  320.6 3.4 %add_divide_fusion = f32[64,5184]{1,0:T(8,128)} fusion(f32[64,5184]{1,0:T(8,128)} %param.8, f32[64,5184]{1,0:T(8,128)} %reshape.18, f32[64,5184]{1,0:T(8,128)} %reduce-scatter.2.cloned.1.call-done, bf16[64,5184]{1,0:T(8,128)(2,1)S(1)} %copy-done.4), kind=kLoop, calls=%fused_computation.8 | loop fusion | flops 1327104 | bytes 5971968 | tf_op jit(solution)/shard_map/div | solution.py:40
  (28 shorter events, 2.0 us)
Async XLA Ops:
  6.5 2.4 copy-start.1
  6.5 41.5 %all-gather.6.cloned.1.call-start = ((), (), s32[]{:S(2)}) async-start(), calls=%async_computation.8 | async-start | bytes 3358720 | tf_op jit(solution)/shard_map/all_gather | solution.py:21
  8.9 64.4 %all-gather.4.cloned.1.call-start = ((), (), s32[]{:S(2)}) async-start(), calls=%async_computation.5 | async-start | bytes 3358720 | tf_op jit(solution)/shard_map/all_gather | solution.py:24
  65.2 8.1 %copy-start.3 = (bf16[64,5184]{1,0:T(8,128)(2,1)S(1)}, bf16[64,5184]{1,0:T(8,128)(2,1)}, u32[]{:S(2)}) copy-start(bf16[64,5184]{1,0:T(8,128)(2,1)} %param.9) | copy-start | bytes 1990660
  65.2 36.5 %all-to-all-start = ((bf16[64,4,5184]{2,0,1:T(8,128)(2,1)}), bf16[64,4,5184]{2,0,1:T(8,128)(2,1)}, u32[]{:S(2)}, u32[]{:S(2)}) async-start(bf16[64,4,5184]{2,0,1:T(8,128)(2,1)} %copy.49), calls=%async_computation | async-start | bytes 5373952 | tf_op jit(solution)/shard_map/all_to_all | solution.py:22
  69.9 57.6 %all-reduce.2.cloned.1.call-start = ((), (), s32[]{:S(2)}) async-start(), calls=%async_computation.6 | async-start | bytes 131072 | tf_op jit(solution)/shard_map/psum | solution.py:26
  76.6 244.0 %reduce-scatter.2.cloned.1.call-start = ((), (), s32[]{:S(2)}) async-start(), calls=%async_computation.7 | async-start | bytes 6717440 | tf_op jit(solution)/shard_map/reduce_scatter | solution.py:31
  101.6 25.9 %copy-start = (bf16[64,5184]{1,0:T(8,128)(2,1)S(1)}, bf16[64,5184]{1,0:T(8,128)(2,1)}, u32[]{:S(2)}) copy-start(bf16[64,5184]{1,0:T(8,128)(2,1)} %convert_element_type.13) | copy-start | bytes 1990660
  152.7 19.0 %slice-start = ((s8[4718592]{0:T(1024)(128)(4,1)}), s8[524288]{0:T(1024)(128)(4,1)S(1)}, s32[]{:S(2)}) async-start(s8[4718592]{0:T(1024)(128)(4,1)} %bitcast.61), calls=%async_computation.9 | async-start | bytes 1048576
  162.0 9.7 %slice-start.1 = ((s8[4718592]{0:T(1024)(128)(4,1)}), s8[4194304]{0:T(1024)(128)(4,1)S(1)}, s32[]{:S(2)}) async-start(s8[4718592]{0:T(1024)(128)(4,1)} %bitcast.61), calls=%async_computation.10 | async-start | bytes 8388608
  162.1 9.7 %copy-start.2 = (bf16[4,16,144,144,1]{3,2,1,0,4:T(8,128)(2,1)S(1)}, bf16[4,16,144,144,1]{3,2,1,0,4:T(8,128)(2,1)}, u32[]{:S(2)}) copy-start(bf16[4,16,144,144,1]{3,2,1,0,4:T(8,128)(2,1)} %reshape.22) | copy-start | bytes 7962628
  318.4 2.2 copy-start.4
Sparse Core Ops, SparseCore 0:
  9.1 38.8 all-gather.5
  49.5 23.6 all-gather.3
  76.8 34.1 all-reduce.1
  133.5 46.5 reduce-scatter.1
where the time goes:
time: 336 us; the launch traced here: 331 us
  local copies, waits for them, and re-layouts  94 us (28%)
  blocking collectives  83.5 us (25%)
  waiting for transfers between devices  66.2 us (20%)
  matrix products  51.8 us (15%)
  other arithmetic  16.7 us (5%)
  between operations  13.4 us (4%)
  starting transfers between devices  5.01 us (1%)
    all_gather x1, waiting for transfers between devices, local_sweep(): t_rows = lax.all_gather(t_half, 'col', axis=1, tiled=True)  38 us
    all_to_all x1, blocking collectives, local_sweep(): swap_row = lax.all_to_all(ph_back, 'row', 1, 0, tiled=True)  31 us
    all_to_all x1, blocking collectives, local_sweep(): ph_back = lax.all_to_all(direct_term - exch_term, 'col', 2, 1, tiled=True)  30.8 us
    dot_general x1, matrix products, local_sweep(): jnp.dot(t_ladder, vvvv_blk, preferred_element_type=jnp.float32)  25.9 us
    all_to_all x1, waiting for transfers between devices, local_sweep(): t_ladder = lax.all_to_all(t_rows, 'row', 1, 0, tiled=True)  24.8 us
    all_to_all x1, blocking collectives, local_sweep(): swap_both = lax.all_to_all(swap_row, 'col', 3, 2, tiled=True)  21.8 us
    unnamed x17, local copies, waits for them, and re-layouts  21.4 us
    all_to_all x3, local copies, waits for them, and re-layouts, local_sweep(): swap_both = lax.all_to_all(swap_row, 'col', 3, 2, tiled=True)  13.5 us
  transfers between devices with their start and end apart: 5, of which 3 were waited for; matrix products, arithmetic and copies ran while one was open for 43% of the time, Pallas kernels for 0%

commit v1 on v0

v1 whole, which is shorter than its diff:
```python
import functools
import math

import jax
import jax.numpy as jnp
from jax import lax
from jax.experimental import pallas as pl
from jax.experimental.pallas import tpu as pltpu
from jax.sharding import PartitionSpec as P

F32 = jnp.float32
BF16 = jnp.bfloat16
MESH = pl.DeviceIdType.MESH
CHUNK = 512
LANES = 128
NQ = 4


def sweep_kernel(
    dims,
    t_hbm, den_hbm, oovv_hbm, vvvv_hbm, vlast_hbm, oooo_hbm, wd_hbm, wx_hbm, perm_hbm, swap_hbm,
    out_hbm,
    t32, rows, lad, tcols, wd, wx, wxt, tr, r3, r5, sd, sp, msg_d, msg_p, got_d, got_p,
    part, half, xsend, xgot, vbuf, vlast, oovv, oooo, perm, swap, xpart, xgot_part, m_mine, m_got,
    in_sem, vb_sem, loc_sem, ts_sem, tr_sem, ls_sem, lr_sem, g_sem,
    ps_sem, pr_sem, d_sem, hs_sem, hr_sem, xs_sem, xr_sem, x_sem, m_sem,
):
    n_occ, n_virt, n_row, n_col = dims
    rows_dev, cols_dev = t32.shape
    occ = n_occ // n_row
    vir = n_virt // n_col
    qrows = rows_dev // NQ
    n_full = cols_dev // CHUNK
    tail = cols_dev - n_full * CHUNK
    r = lax.axis_index("row")
    c = lax.axis_index("col")
    x, u = r // 2, r % 2
    z, y = c // 2, c % 2
    c_y, c_z, c_d = 2 * z + 1 - y, 2 * (1 - z) + y, 2 * (1 - z) + 1 - y
    r_p, r_s, r_o = 2 * x + 1 - u, 2 * (1 - x) + u, 2 * (1 - x) + 1 - u
    col_peers = (c_y, c_z, c_d)
    row_peers = (r_p, r_s, r_o)

    def remote(src, dst, ssem, rsem, row, col):
        return pltpu.make_async_remote_copy(
            src_ref=src, dst_ref=dst, send_sem=ssem, recv_sem=rsem,
            device_id={"row": row, "col": col}, device_id_type=MESH)

    def load(src, dst, k):
        return pltpu.make_async_copy(src, dst, in_sem.at[k])

    ld_t = load(t_hbm, t32, 0)
    ld_wx = load(wx_hbm, wx, 1)
    ld_wd = load(wd_hbm, wd, 2)
    ld_oovv = load(oovv_hbm, oovv, 3)
    ld_oooo = load(oooo_hbm, oooo, 4)
    ld_perm = load(perm_hbm, perm, 5)
    ld_swap = load(swap_hbm, swap, 6)
    ld_den = load(den_hbm, t32, 7)
    for ld in (ld_t, ld_wx, ld_wd, ld_oovv, ld_oooo, ld_perm, ld_swap):
        ld.start()

    def fetch(off, width, slot):
        return pltpu.make_async_copy(vvvv_hbm.at[:, pl.ds(off, width)], vbuf.at[slot], vb_sem.at[slot])

    for s in range(2):
        fetch(s * CHUNK, CHUNK, s).start()
    ld_last = load(vlast_hbm, vlast, 9)
    ld_last.start()

    barrier = pltpu.get_barrier_semaphore()
    for p in col_peers:
        pl.semaphore_signal(barrier, inc=1, device_id={"row": r, "col": p}, device_id_type=MESH)
    for p in row_peers:
        pl.semaphore_signal(barrier, inc=1, device_id={"row": p, "col": c}, device_id_type=MESH)
    pl.semaphore_wait(barrier, 6)

    def piece(ref, k, q):
        return ref.at[k, pl.ds(q * qrows, qrows), :]

    def send_y(q):
        return remote(piece(rows, c, q), piece(rows, c, q), ts_sem.at[0, q], tr_sem.at[0, q], r, c_y)

    def send_z(q):
        return remote(piece(rows, c, q), piece(rows, c, q), ts_sem.at[1, q], tr_sem.at[1, q], r, c_z)

    def send_d(q):
        return remote(piece(rows, c_y, q), piece(rows, c_y, q), ts_sem.at[2, q], tr_sem.at[2, q], r, c_z)

    blk_x = 2 * (1 - x) + y

    def send_lx(q):
        return remote(piece(rows, blk_x, q), piece(lad, r, q), ls_sem.at[0, q], lr_sem.at[u, q], blk_x, c)

    def recv_lx(w, q):
        k = 2 * (1 - x) + w
        return remote(piece(lad, k, q), piece(lad, k, q), ls_sem.at[0, q], lr_sem.at[w, q], blk_x, c)

    def send_ly(w, q):
        k = 2 * (1 - x) + w
        return remote(piece(lad, k, q), piece(lad, k, q), ls_sem.at[1 + w, q], lr_sem.at[2 + w, q], r, c_y)

    own_ladder = z == 1 - x
    direct = u == y

    ld_t.wait()
    for q in range(NQ):
        rows[c, pl.ds(q * qrows, qrows), :] = t32[pl.ds(q * qrows, qrows), :].astype(BF16)
        send_y(q).start()
        send_z(q).start()

        @pl.when(own_ladder)
        def _():
            send_lx(q).start()

    ld_den.start()

    def row_send(k, p):
        return remote(rows.at[c], tcols.at[r], g_sem.at[0, k], g_sem.at[1, k], p, c)

    for k, p in enumerate(row_peers):
        row_send(k, p).start()

    tcols[r] = rows[c]

    ld_wx.wait()

    @pl.loop(0, wx.shape[0] // 128)
    def _(m):
        src = pl.ds(pl.multiple_of(m * 128, 128), 128)
        for b in range(0, wx.shape[1], 128):
            w = min(128, wx.shape[1] - b)
            wxt[b:b + w, src] = wx[src, b:b + w].astype(F32).T.astype(BF16)

    def forward_ladder(q):
        @pl.when(direct)
        def _():
            for w in range(2):
                recv_lx(w, q).wait_recv()
                send_ly(w, q).start()

    for q in range(NQ):
        send_z(q).wait_recv()

        @pl.when(jnp.logical_not(own_ladder))
        def _():
            send_lx(q).start()

        send_y(q).wait_recv()
        send_d(q).start()
        if q:
            forward_ladder(q - 1)
    forward_ladder(NQ - 1)
    for q in range(NQ):
        send_d(q).wait_recv()

    lad_p = remote(rows.at[r_p], lad.at[r], g_sem.at[0, 3], g_sem.at[1, 3], r_p, c)
    lad_p.start()
    lad[r] = rows[r]

    for k, p in enumerate(row_peers):
        row_send(k, p).wait_recv()
    ld_oovv.wait()
    for k in range(n_row):
        xpart[:, k * rows_dev:(k + 1) * rows_dev] = lax.dot_general(
            oovv[...], tcols[k], (((1,), (1,)), ((), ())), preferred_element_type=F32)

    def x_send(k, p):
        return remote(xpart, xgot_part.at[c], x_sem.at[0, k], x_sem.at[1, k], r, p)

    for k, p in enumerate(col_peers):
        x_send(k, p).start()

    ld_swap.wait()
    ld_wd.wait()

    @pl.loop(0, occ)
    def _(i):
        lines = pl.ds(pl.multiple_of(i * n_occ, n_occ), n_occ)
        for ab in range(n_virt // n_occ):
            stack = []
            for t in range(n_occ):
                a = ab * n_occ + t
                lo = (a % vir) * n_virt
                stack.append(rows[a // vir, lines, lo:lo + n_virt])
            turned = jnp.dot(swap[...], jnp.concatenate(stack, axis=0), preferred_element_type=F32).astype(BF16)
            for k in range(n_occ):
                tr[i, k * n_virt + ab * n_occ:k * n_virt + (ab + 1) * n_occ, :] = turned[k * n_occ:(k + 1) * n_occ]

        r5[...] = jnp.dot(wxt[...], tr[i], preferred_element_type=F32)
        r3[...] = jnp.dot(tr[i, 0:n_virt, :], wd[0:n_virt, :], preferred_element_type=F32)

        @pl.loop(1, n_occ)
        def _(k):
            at = pl.ds(pl.multiple_of(k * n_virt, 16), n_virt)
            r3[...] += jnp.dot(tr[i, at, :], wd[at, :], preferred_element_type=F32)

        for j in range(occ):
            diff = r3[:, j * n_virt:(j + 1) * n_virt] - r5[j * n_virt:(j + 1) * n_virt, :]
            sd[i * occ + j] = diff
            sp[j * occ + i] = diff.T

    n_pair = occ * occ
    pad = pl.ds(cols_dev - tail, LANES)
    for k in range(n_col):
        msg_p[k, :, pad] = jnp.zeros((n_pair, LANES), F32)
        msg_d[k, :, pad] = jnp.zeros((n_pair, LANES), F32)
        part[k, :, pad] = jnp.zeros((rows_dev, LANES), F32)

    @pl.loop(0, n_col)
    def _(k):
        for a in range(vir):
            msg_p[k, :, a * n_virt:(a + 1) * n_virt] = sp[:, k * vir + a, :]

    def p_send(off, width, n, k, p):
        at = pl.ds(off, width)
        return remote(msg_p.at[p, :, at], got_p.at[c, :, at], ps_sem.at[k, n], pr_sem.at[k, n], r, p)

    chunks = [(n * CHUNK, CHUNK) for n in range(n_full)] + [(n_full * CHUNK, LANES)]
    for n, (off, width) in enumerate(chunks):
        for k, p in enumerate(col_peers):
            p_send(off, width, n, k, p).start()
    own_p = pltpu.make_async_copy(msg_p.at[c], got_p.at[c], loc_sem.at[0])
    own_p.start()

    @pl.loop(0, n_col)
    def _(k):
        for a in range(vir):
            msg_d[k, :, a * n_virt:(a + 1) * n_virt] = sd[:, k * vir + a, :]

    def d_send(k, p):
        return remote(msg_d.at[p], got_d.at[c], d_sem.at[0, k], d_sem.at[1, k], r, p)

    for k, p in enumerate(col_peers):
        d_send(k, p).start()
    own_d = pltpu.make_async_copy(msg_d.at[c], got_d.at[c], loc_sem.at[1])
    own_d.start()

    for k, p in enumerate(col_peers):
        x_send(k, p).wait_recv()
    xgot_part[c] = xpart[...]
    x_sum = xgot_part[0] + xgot_part[1] + xgot_part[2] + xgot_part[3]
    ld_oooo.wait()
    hole = (oooo[pl.ds(pl.multiple_of(r * rows_dev, rows_dev), rows_dev), :].astype(F32) + 0.5 * x_sum)
    for k in range(n_row):
        m_mine[k] = hole[:, k * rows_dev:(k + 1) * rows_dev].astype(BF16)

    def m_send(k, p):
        return remote(m_mine.at[p], m_got.at[r], m_sem.at[0, k], m_sem.at[1, k], p, c)

    for k, p in enumerate(row_peers):
        m_send(k, p).start()
    m_got[r] = m_mine[r]

    lad_p.wait_recv()

    @pl.when(jnp.logical_not(direct))
    def _():
        for q in range(NQ):
            for w in range(2):
                send_ly(w, q).wait_recv()

    @pl.when(direct)
    def _():
        for q in range(NQ):
            for w in range(2):
                send_ly(w, q).wait_send()
    lad_p.wait_send()
    ld_perm.wait()

    @pl.loop(0, n_row)
    def _(k):
        for off in range(0, cols_dev, CHUNK):
            width = min(CHUNK, cols_dev - off)
            block = jnp.dot(perm[...], lad[k, :, off:off + width], preferred_element_type=F32)
            lad[k, :, off:off + width] = block.astype(BF16)

    own_p.wait()

    def h_send(off, width, n, w):
        at = pl.ds(off, width)
        return remote(part.at[2 * w + 1 - u, :, at], half.at[w, :, at], hs_sem.at[w, n], hr_sem.at[w, n], r_p, c)

    def x_pass(off, width, n):
        at = pl.ds(off, width)
        return remote(xsend.at[:, at], xgot.at[:, at], xs_sem.at[n], xr_sem.at[n], r_s, c)

    def across(off, width, n):
        at = pl.ds(off, width)
        for w in range(2):
            h_send(off, width, n, w).wait_recv()
        xsend[:, at] = part[2 * (1 - x) + u, :, at] + half[1 - x, :, at]
        x_pass(off, width, n).start()

    def ladder(off, width, n, v_ref):
        at = pl.ds(off, width)
        t_all = lad[...].reshape(n_row * rows_dev, cols_dev)
        prod = jnp.dot(t_all, v_ref[...], preferred_element_type=F32)
        part[:, :, pl.ds(off, prod.shape[1])] = prod.reshape(n_row, rows_dev, prod.shape[1])
        for k, p in enumerate(col_peers):
            p_send(off, width, n, k, p).wait_recv()
        mine = pl.ds(pl.multiple_of(r * n_pair, n_pair), n_pair)
        for k in range(n_col):
            part[k, mine, at] += got_p[k, :, at]
        for w in range(2):
            h_send(off, width, n, w).start()

    @pl.loop(0, n_full)
    def _(n):
        off = pl.multiple_of(n * CHUNK, CHUNK)
        fetch(off, CHUNK, n % 2).wait()
        ladder(off, CHUNK, n, vbuf.at[n % 2])

        @pl.when(n + 2 < n_full)
        def _():
            fetch(pl.multiple_of((n + 2) * CHUNK, CHUNK), CHUNK, n % 2).start()

        @pl.when(n >= 1)
        def _():
            across(pl.multiple_of((n - 1) * CHUNK, CHUNK), CHUNK, n - 1)

    ld_last.wait()
    ladder(n_full * CHUNK, LANES, n_full, vlast)
    across((n_full - 1) * CHUNK, CHUNK, n_full - 1)
    across(n_full * CHUNK, LANES, n_full)

    for k, p in enumerate(row_peers):
        m_send(k, p).wait_recv()
    for k, p in enumerate(col_peers):
        d_send(k, p).wait_recv()
    own_d.wait()
    ld_den.wait()

    def finish(off, width, n):
        at = pl.ds(off, width)
        hole_term = None
        for k in range(n_row):
            term = lax.dot_general(
                m_got[k], tcols[k, :, at], (((0,), (0,)), ((), ())), preferred_element_type=F32)
            hole_term = term if hole_term is None else hole_term + term
        own = part[r, :, at] + half[x, :, at] + xgot[:, at]
        for jh in range(n_col):
            v = own[jh * n_pair:(jh + 1) * n_pair] + got_d[jh, :, at]
            for i in range(occ):
                lo = i * n_occ + jh * occ
                xgot[lo:lo + occ, at] = v[i * occ:(i + 1) * occ]
        total = oovv[:, at].astype(F32) + xgot[:, at] + hole_term
        t32[:, at] = total / t32[:, at]

    @pl.loop(0, n_full)
    def _(n):
        off = pl.multiple_of(n * CHUNK, CHUNK)
        x_pass(off, CHUNK, n).wait_recv()
        finish(off, CHUNK, n)

    x_pass(n_full * CHUNK, LANES, n_full).wait_recv()
    finish(n_full * CHUNK, tail, n_full)
    st = pltpu.make_async_copy(t32, out_hbm, in_sem.at[8])
    st.start()

    for q in range(NQ):
        send_y(q).wait_send()
        send_z(q).wait_send()
        send_d(q).wait_send()
        send_lx(q).wait_send()
    for k, p in enumerate(row_peers):
        row_send(k, p).wait_send()
        m_send(k, p).wait_send()
    for k, p in enumerate(col_peers):
        x_send(k, p).wait_send()
        d_send(k, p).wait_send()
    for n, (off, width) in enumerate(chunks):
        for k, p in enumerate(col_peers):
            p_send(off, width, n, k, p).wait_send()
        for w in range(2):
            h_send(off, width, n, w).wait_send()
        x_pass(off, width, n).wait_send()
    st.wait()


def solution(mesh):
    n_row = mesh.shape["row"]
    n_col = mesh.shape["col"]
    amp_spec = P("row", "col")
    wide_spec = P(None, "col")

    def local_sweep(t_blk, d_blk, oovv_blk, vvvv_blk, oooo_full, wd_blk, wx_blk):
        rows_dev, cols_dev = t_blk.shape
        n_occ = math.isqrt(oooo_full.shape[0])
        n_virt = wd_blk.shape[0] // n_occ
        occ, vir = n_occ // n_row, n_virt // n_col
        n_pair = occ * occ
        n_chunk = cols_dev // CHUNK + 1
        v_last = vvvv_blk[:, cols_dev // CHUNK * CHUNK:]
        wide = -(-cols_dev // LANES) * LANES
        kc, jb = wd_blk.shape
        perm = jnp.eye(rows_dev, dtype=BF16).reshape(occ, n_col, occ, rows_dev).transpose(1, 0, 2, 3).reshape(rows_dev, rows_dev)
        n_sq = n_occ * n_occ
        swap = jnp.eye(n_sq, dtype=BF16).reshape(n_occ, n_occ, n_sq).transpose(1, 0, 2).reshape(n_sq, n_sq)
        dma = pltpu.SemaphoreType.DMA
        vm = pltpu.VMEM
        hbm = pl.BlockSpec(memory_space=pl.ANY)
        block = (rows_dev, cols_dev)
        return pl.pallas_call(
            functools.partial(sweep_kernel, (n_occ, n_virt, n_row, n_col)),
            out_shape=jax.ShapeDtypeStruct(block, F32),
            in_specs=[hbm] * 10,
            out_specs=hbm,
            scratch_shapes=[
                vm(block, F32), vm((n_col,) + block, BF16), vm((n_row,) + block, BF16), vm((n_row,) + block, BF16),
                vm((kc, jb), BF16), vm((kc, jb), BF16), vm((jb, kc), BF16),
                vm((occ, kc, n_virt), BF16), vm((n_virt, jb), F32), vm((jb, n_virt), F32),
                vm((n_pair, n_virt, n_virt), F32), vm((n_pair, n_virt, n_virt), F32),
                vm((n_col, n_pair, wide), F32), vm((n_col, n_pair, wide), F32),
                vm((n_col, n_pair, wide), F32), vm((n_col, n_pair, wide), F32),
                vm((n_row, rows_dev, wide), F32), vm((2, rows_dev, wide), F32),
                vm((rows_dev, wide), F32), vm((rows_dev, wide), F32),
                vm((2, cols_dev, CHUNK), BF16), vm(v_last.shape, BF16), vm(block, BF16), vm(oooo_full.shape, BF16),
                vm((rows_dev, rows_dev), BF16), vm((n_sq, n_sq), BF16),
                vm((rows_dev, n_sq), F32), vm((n_col, rows_dev, n_sq), F32),
                vm((n_row, rows_dev, rows_dev), BF16), vm((n_row, rows_dev, rows_dev), BF16),
                dma((10,)), dma((2,)), dma((2,)), dma((3, NQ)), dma((3, NQ)), dma((3, NQ)), dma((4, NQ)), dma((2, 4)),
                dma((3, n_chunk)), dma((3, n_chunk)), dma((2, 3)), dma((2, n_chunk)), dma((2, n_chunk)),
                dma((n_chunk,)), dma((n_chunk,)), dma((2, 3)), dma((2, 3)),
            ],
            compiler_params=pltpu.CompilerParams(
                collective_id=0, has_side_effects=True, vmem_limit_bytes=67043328),
        )(t_blk, d_blk, oovv_blk, vvvv_blk, v_last, oooo_full, wd_blk, wx_blk, perm, swap)

    return jax.shard_map(
        local_sweep, mesh=mesh,
        in_specs=(amp_spec, amp_spec, amp_spec, amp_spec, P(), wide_spec, wide_spec),
        out_specs=amp_spec, check_vma=False)
```

time: 336 us -> 128 us (0.38); the launches traced: 331 us -> 128 us
  Pallas kernels: 0 us -> 114 us
  blocking collectives: 83.5 us -> 0 us
  local copies, waits for them, and re-layouts: 94 us -> 12.6 us
  waiting for transfers between devices: 66.2 us -> 0 us
  matrix products: 51.8 us -> 0 us
  other arithmetic: 16.7 us -> 1.45 us
  between operations: 13.4 us -> 0.02 us
  starting transfers between devices: 5.01 us -> 0 us
    pallas_call x0 -> x1, Pallas kernels: none -> 114 us  [local_sweep(): pl.pallas_call(functools.partial(sweep_kernel, (n_occ, n_virt, n_row, n_c...]
    all_to_all x3 -> x0, blocking collectives: 83.5 us -> none  [the longest x1 31 us: local_sweep(): swap_row = lax.all_to_all(ph_back, 'row', 1, 0, tiled=True)]
    dot_general x5 -> x0, matrix products: 51.8 us -> none  [the longest x1 25.9 us: local_sweep(): jnp.dot(t_ladder, vvvv_blk, preferred_element_type=jnp.float32)]
    all_gather x2 -> x0, waiting for transfers between devices: 41.4 us -> none  [the longest x1 38 us: local_sweep(): t_rows = lax.all_gather(t_half, 'col', axis=1, tiled=True)]
    all_to_all x8 -> x0, local copies, waits for them, and re-layouts: 32.7 us -> none  [the longest x3 13.5 us: local_sweep(): swap_both = lax.all_to_all(swap_row, 'col', 3, 2, tiled=True)]
    reshape x4 -> x0, local copies, waits for them, and re-layouts: 30.8 us -> none  [the longest x1 9.68 us: local_sweep(): wx_blk.reshape(n_occ, n_virt, occ_col, n_virt)]
    all_to_all x1 -> x0, waiting for transfers between devices: 24.8 us -> none  [local_sweep(): t_ladder = lax.all_to_all(t_rows, 'row', 1, 0, tiled=True)]
    unnamed x17 -> x5, local copies, waits for them, and re-layouts: 21.4 us -> 9.94 us
  transfers between devices with their start and end apart: 5 -> 0, of which waited for: 3 -> 0; matrix products, arithmetic and copies ran while one was open for 43% -> 0% of each run, Pallas kernels for 0% -> 0%
where the time goes in v1:
time: 128 us
  Pallas kernels  114 us (89%)
  local copies, waits for them, and re-layouts  12.6 us (10%)
  other arithmetic  1.45 us (1%)
    pallas_call x1, Pallas kernels, local_sweep(): pl.pallas_call(functools.partial(sweep_kernel, (n_occ, n_virt, n_row, n_c...  114 us
    unnamed x5, local copies, waits for them, and re-layouts  9.94 us

profile of v1, /device:TPU:0, one launch (start us, length us, event | category | flops | bytes accessed | tf_op | source)
XLA Modules:
  0.0 127.7 jit_solution(12056153502984452513)
XLA Ops:
  0.0 0.0 copy-start
  0.0 0.1 iota.94
  0.1 0.1 iota.102
  0.2 0.7 fusion.1.perm_hbm
  0.9 0.8 fusion.swap_hbm
  1.6 2.5 %slice.3.vlast_hbm = bf16[5184,64]{1,0:T(8,128)(2,1)} slice(bf16[5184,5184]{1,0:T(8,128)(2,1)} %vvvv_hbm.1), slice={[0:5184], [5120:5184]} | slice | bytes 1327104 | tf_op jit(solution)/shard_map/slice | solution.py:394
  4.1 0.0 copy-done
  4.1 2.9 %copy.8.wd_hbm = bf16[2304,576]{1,0:T(8,128)(2,1)} copy(bf16[2304,576]{0,1:T(8,128)(2,1)S(1)} %copy-done) | data formatting | bytes 5308416 | tf_op args[5]
  7.0 4.5 %copy.9.wx_hbm = bf16[2304,576]{1,0:T(8,128)(2,1)} copy(bf16[2304,576]{0,1:T(8,128)(2,1)} %param.13) | data formatting | bytes 5308416 | tf_op args[6]
  11.6 113.6 %shard_map.73 = f32[64,5184]{1,0:T(8,128)} custom-call(f32[64,5184]{1,0:T(8,128)} %t_hbm.1, f32[64,5184]{1,0:T(8,128)} %den_hbm.1, bf16[64,5184]{1,0:T(8,128)(2,1)} %oovv_hbm.1, bf16[5184,5184]{1,0:T(8,128)(2,1)} %vvvv_hbm.1, bf16[5184,64]{1,0:T(8,128)(2,1)} %slice.3.vlast_hbm, bf16[256,256]{1,0:T(8,128)(2,1)} %oooo_hbm.1, bf16[2304,576]{1,0:T(8,128)(2,1)} %copy.8.wd_hbm, ...), custom_call_target="tpu_custom_call" | custom-call | tf_op jit(solution)/shard_map/pallas_call | solution.py:404
  125.2 2.5 %copy.11 = f32[64,5184]{1,0:T(8,128)} copy(f32[64,5184]{1,0:T(8,128)} %shard_map.73) | data formatting | bytes 2654208
  (2 shorter events, 0.0 us)
Async XLA Ops:
  0.0 4.1 %copy-start = (bf16[2304,576]{0,1:T(8,128)(2,1)S(1)}, bf16[2304,576]{0,1:T(8,128)(2,1)}, u32[]{:S(2)}) copy-start(bf16[2304,576]{0,1:T(8,128)(2,1)} %param.12) | copy-start | bytes 7962628

commit v2 on v1

v2 whole, which is shorter than its diff:
```python
import functools
import math

import jax
import jax.numpy as jnp
import numpy as np
from jax import lax
from jax.experimental import pallas as pl
from jax.experimental.pallas import tpu as pltpu
from jax.sharding import PartitionSpec as P

F32 = jnp.float32
BF16 = jnp.bfloat16
MESH = pl.DeviceIdType.MESH
CHUNK = 512
LANES = 128
P_AHEAD = 3
AHEAD = 2
OVER_Y = 1
FORWARD = ((2, (0,)), (3, (1,)), (4, (2, 3)))
NQ = 4


def sweep_kernel(
    dims,
    t_hbm, den_hbm, oovv_hbm, vvvv_hbm, vlast, oooo_hbm, wd_hbm, wx_hbm, perm_hbm, swap_hbm,
    out_hbm,
    t32, rows, lad, tcols, wd, wdt, wxt, tr, ta, r3, r5, sd, sp, msg_d, msg_p, got_d, got_p,
    part, half, xsend, xgot, vbuf, oovv, oooo, perm, swap, xpart, xgot_part, m_mine, m_got,
    in_sem, vb_sem, loc_sem, ts_sem, tr_sem, ls_sem, lr_sem, g_sem,
    rx_sem, ps_sem, pr_sem, d_sem, hs_sem, hr_sem, xs_sem, xr_sem, x_sem, m_sem,
):
    n_occ, n_virt, n_row, n_col = dims
    rows_dev, cols_dev = t32.shape
    occ = n_occ // n_row
    vir = n_virt // n_col
    qrows = rows_dev // NQ
    n_full = cols_dev // CHUNK
    tail = cols_dev - n_full * CHUNK
    r = lax.axis_index("row")
    c = lax.axis_index("col")
    x, u = r // 2, r % 2
    z, y = c // 2, c % 2
    c_y, c_z, c_d = 2 * z + 1 - y, 2 * (1 - z) + y, 2 * (1 - z) + 1 - y
    r_p, r_s, r_o = 2 * x + 1 - u, 2 * (1 - x) + u, 2 * (1 - x) + 1 - u
    col_peers = (c_y, c_z, c_d)
    row_peers = (r_p, r_s, r_o)

    def remote(src, dst, ssem, rsem, row, col):
        return pltpu.make_async_remote_copy(
            src_ref=src, dst_ref=dst, send_sem=ssem, recv_sem=rsem,
            device_id={"row": row, "col": col}, device_id_type=MESH)

    def load(src, dst, k):
        return pltpu.make_async_copy(src, dst, in_sem.at[k])

    ld_t = load(t_hbm, t32, 0)
    ld_wx = load(wx_hbm, wxt, 1)
    ld_wd = load(wd_hbm, wdt, 2)
    ld_oovv = load(oovv_hbm, oovv, 3)
    ld_oooo = load(oooo_hbm, oooo, 4)
    ld_perm = load(perm_hbm, perm, 5)
    ld_swap = load(swap_hbm, swap, 6)
    ld_den = load(den_hbm, t32, 7)
    for ld in (ld_t, ld_wx, ld_wd, ld_oovv, ld_oooo, ld_perm, ld_swap):
        ld.start()

    def fetch(off, width, slot):
        return pltpu.make_async_copy(vvvv_hbm.at[:, pl.ds(off, width)], vbuf.at[slot], vb_sem.at[slot])

    for s in range(2):
        fetch(s * CHUNK, CHUNK, s).start()

    barrier = pltpu.get_barrier_semaphore()
    for p in col_peers:
        pl.semaphore_signal(barrier, inc=1, device_id={"row": r, "col": p}, device_id_type=MESH)
    for p in row_peers:
        pl.semaphore_signal(barrier, inc=1, device_id={"row": p, "col": c}, device_id_type=MESH)
    pl.semaphore_wait(barrier, 6)

    def piece(ref, k, q):
        return ref.at[k, pl.ds(pl.multiple_of(q * qrows, qrows), qrows), :]

    def send_y(q):
        return remote(piece(rows, c, q), piece(rows, c, q), ts_sem.at[0, q], tr_sem.at[0, q], r, c_y)

    def send_z(q):
        return remote(piece(rows, c, q), piece(rows, c, q), ts_sem.at[1, q], tr_sem.at[1, q], r, c_z)

    def send_dz(q):
        return remote(piece(rows, c_y, q), piece(rows, c_y, q), ts_sem.at[2, q], tr_sem.at[2, q], r, c_z)

    def send_dy(q):
        return remote(piece(rows, c_z, q), piece(rows, c_z, q), ts_sem.at[2, q], tr_sem.at[2, q], r, c_y)

    blk_x = 2 * (1 - x) + y

    def send_lx(q):
        return remote(piece(rows, blk_x, q), piece(lad, r, q), ls_sem.at[0, q], lr_sem.at[u, q], blk_x, c)

    def recv_lx(w, q):
        k = 2 * (1 - x) + w
        return remote(piece(lad, k, q), piece(lad, k, q), ls_sem.at[0, q], lr_sem.at[w, q], blk_x, c)

    def send_ly(w, q):
        k = 2 * (1 - x) + w
        return remote(piece(lad, k, q), piece(lad, k, q), ls_sem.at[1 + w, q], lr_sem.at[2 + w, q], r, c_y)

    own_ladder = z == 1 - x
    direct = u == y

    ld_t.wait()
    for q in range(NQ):
        rows[c, pl.ds(q * qrows, qrows), :] = t32[pl.ds(q * qrows, qrows), :].astype(BF16)
        if q < AHEAD:
            send_y(q).start()
            send_z(q).start()

            @pl.when(own_ladder)
            def _():
                send_lx(q).start()

    ld_den.start()

    def send_row(q):
        return remote(piece(rows, c, q), piece(tcols, r, q), rx_sem.at[0, q], rx_sem.at[1, q], r_s, c)

    row_p = remote(rows.at[c], tcols.at[r], g_sem.at[0, 0], g_sem.at[1, 0], r_p, c)
    row_o = remote(tcols.at[r_s], tcols.at[r_s], g_sem.at[0, 1], g_sem.at[1, 1], r_p, c)
    row_p.start()
    send_row(0).start()
    tcols[r] = rows[c]

    with jax.named_scope("ph_turn_w"):
        ld_wd.wait()

        @pl.loop(0, wd.shape[0] // LANES)
        def _(m):
            at = pl.ds(pl.multiple_of(m * LANES, LANES), LANES)
            for b in range(0, wd.shape[1], LANES):
                w = min(LANES, wd.shape[1] - b)
                wd[at, b:b + w] = wdt[b:b + w, at].astype(F32).T.astype(BF16)

    def forward_ladder(q):
        @pl.when(direct)
        def _():
            for w in range(2):
                recv_lx(w, q).wait_recv()
                send_ly(w, q).start()

    ld_swap.wait()
    ld_wx.wait()

    def spread(i):
        lines = pl.ds(pl.multiple_of(i * n_occ, n_occ), n_occ)
        for ab in range(n_virt // n_occ):
            stack = []
            for t in range(n_occ):
                a = ab * n_occ + t
                lo = (a % vir) * n_virt
                stack.append(rows[a // vir, lines, lo:lo + n_virt])
            turned = jnp.dot(swap[...], jnp.concatenate(stack, axis=0), preferred_element_type=F32).astype(BF16)
            for k in range(n_occ):
                line = turned[k * n_occ:(k + 1) * n_occ]
                tr[k * n_virt + ab * n_occ:k * n_virt + (ab + 1) * n_occ, :] = line
                ta[ab * n_occ:(ab + 1) * n_occ, k * n_virt:(k + 1) * n_virt] = line

    def particle_hole(i):
        with jax.named_scope("ph_spread"):
            spread(i)
        with jax.named_scope("ph_r5"):
            r5[...] = jnp.dot(wxt[...], tr[...], preferred_element_type=F32)
        with jax.named_scope("ph_r3"):
            r3[...] = jnp.dot(ta[...], wd[...], preferred_element_type=F32)
        with jax.named_scope("ph_diff"):
            for j in range(occ):
                diff = r3[:, j * n_virt:(j + 1) * n_virt] - r5[j * n_virt:(j + 1) * n_virt, :]
                sd[i * occ + j] = diff
                sp[j * occ + i] = diff.T

    @pl.loop(0, NQ + 1)
    def _(q):
        @pl.when(q < NQ)
        def _():
            send_z(q).wait_recv()

            @pl.when(jnp.logical_not(own_ladder))
            def _():
                send_lx(q).start()

            send_y(q).wait_recv()

            @pl.when(q == OVER_Y)
            def _():
                send_dy(q).start()

            @pl.when(q != OVER_Y)
            def _():
                send_dz(q).start()

        @pl.when(q + AHEAD < NQ)
        def _():
            send_y(q + AHEAD).start()
            send_z(q + AHEAD).start()

            @pl.when(own_ladder)
            def _():
                send_lx(q + AHEAD).start()

        @pl.when(q + 1 < NQ)
        def _():
            send_row(q + 1).start()

        for at, pieces in FORWARD:
            @pl.when(q == at)
            def _():
                for w in pieces:
                    forward_ladder(w)

        @pl.when(q >= 1)
        def _():
            send_dz(q - 1).wait_recv()
            particle_hole(q - 1)

    lad_p = remote(rows.at[r_p], lad.at[r], g_sem.at[0, 3], g_sem.at[1, 3], r_p, c)
    lad_p.start()
    lad[r] = rows[r]

    n_pair = occ * occ
    pad = pl.ds(cols_dev - tail, LANES)
    for k in range(n_col):
        msg_p[k, :, pad] = jnp.zeros((n_pair, LANES), F32)
        msg_d[k, :, pad] = jnp.zeros((n_pair, LANES), F32)
        part[k, :, pad] = jnp.zeros((rows_dev, LANES), F32)

    @pl.loop(0, n_col)
    def _(k):
        for a in range(vir):
            msg_p[k, :, a * n_virt:(a + 1) * n_virt] = sp[:, k * vir + a, :]

    def p_send(off, width, n, k, p):
        at = pl.ds(off, width)
        return remote(msg_p.at[p, :, at], got_p.at[c, :, at], ps_sem.at[k, n], pr_sem.at[k, n], r, p)

    chunks = [(n * CHUNK, CHUNK) for n in range(n_full)] + [(n_full * CHUNK, LANES)]
    for n, (off, width) in enumerate(chunks[:P_AHEAD]):
        for k, p in enumerate(col_peers):
            p_send(off, width, n, k, p).start()
    own_p = pltpu.make_async_copy(msg_p.at[c], got_p.at[c], loc_sem.at[0])
    own_p.start()

    def d_send(k, p):
        return remote(msg_d.at[p], got_d.at[c], d_sem.at[0, k], d_sem.at[1, k], r, p)

    own_d = pltpu.make_async_copy(msg_d.at[c], got_d.at[c], loc_sem.at[1])

    def form_d():
        @pl.loop(0, n_col)
        def _(k):
            for a in range(vir):
                msg_d[k, :, a * n_virt:(a + 1) * n_virt] = sd[:, k * vir + a, :]

        for k, p in enumerate(col_peers):
            d_send(k, p).start()
        own_d.start()

    lad_p.wait_recv()

    @pl.when(jnp.logical_not(direct))
    def _():
        for q in range(NQ):
            for w in range(2):
                send_ly(w, q).wait_recv()

    @pl.when(direct)
    def _():
        for q in range(NQ):
            for w in range(2):
                send_ly(w, q).wait_send()
    lad_p.wait_send()
    ld_perm.wait()

    @pl.loop(0, n_row)
    def _(k):
        for off in range(0, cols_dev, CHUNK):
            width = min(CHUNK, cols_dev - off)
            block = jnp.dot(perm[...], lad[k, :, off:off + width], preferred_element_type=F32)
            lad[k, :, off:off + width] = block.astype(BF16)

    own_p.wait()

    for q in range(NQ):
        send_row(q).wait_recv()
    row_o.start()

    def h_send(off, width, n, w):
        at = pl.ds(off, width)
        return remote(part.at[2 * w + 1 - u, :, at], half.at[w, :, at], hs_sem.at[w, n], hr_sem.at[w, n], r_p, c)

    def x_pass(off, width, n):
        at = pl.ds(off, width)
        return remote(xsend.at[:, at], xgot.at[:, at], xs_sem.at[n], xr_sem.at[n], r_s, c)

    def across(off, width, n):
        at = pl.ds(off, width)
        with jax.named_scope("ph_wait_h"):
            for w in range(2):
                h_send(off, width, n, w).wait_recv()
        xsend[:, at] = part[2 * (1 - x) + u, :, at] + half[1 - x, :, at]
        x_pass(off, width, n).start()

    def ladder(off, width, n, v_ref):
        at = pl.ds(off, width)
        with jax.named_scope("ph_dot"):
            t_all = lad[...].reshape(n_row * rows_dev, cols_dev)
            prod = jnp.dot(t_all, v_ref[:, 0:min(width, cols_dev - off) if width == LANES else width], preferred_element_type=F32)
            part[:, :, pl.ds(off, prod.shape[1])] = prod.reshape(n_row, rows_dev, prod.shape[1])
        with jax.named_scope("ph_wait_p"):
            for k, p in enumerate(col_peers):
                p_send(off, width, n, k, p).wait_recv()
        mine = pl.ds(pl.multiple_of(r * n_pair, n_pair), n_pair)
        for k in range(n_col):
            part[k, mine, at] += got_p[k, :, at]
        for w in range(2):
            h_send(off, width, n, w).start()

    def x_send(k, p):
        return remote(xpart, xgot_part.at[c], x_sem.at[0, k], x_sem.at[1, k], r, p)

    def form_x():
        row_p.wait_recv()
        row_o.wait_recv()
        ld_oovv.wait()
        for k in range(n_row):
            xpart[:, k * rows_dev:(k + 1) * rows_dev] = lax.dot_general(
                oovv[...], tcols[k], (((1,), (1,)), ((), ())), preferred_element_type=F32)
        for k, p in enumerate(col_peers):
            x_send(k, p).start()

    def m_send(k, p):
        return remote(m_mine.at[p], m_got.at[r], m_sem.at[0, k], m_sem.at[1, k], p, c)

    def form_m():
        for k, p in enumerate(col_peers):
            x_send(k, p).wait_recv()
        xgot_part[c] = xpart[...]
        x_sum = xgot_part[0] + xgot_part[1] + xgot_part[2] + xgot_part[3]
        ld_oooo.wait()
        hole = (oooo[pl.ds(pl.multiple_of(r * rows_dev, rows_dev), rows_dev), :].astype(F32) + 0.5 * x_sum)
        for k in range(n_row):
            m_mine[k] = hole[:, k * rows_dev:(k + 1) * rows_dev].astype(BF16)
        for k, p in enumerate(row_peers):
            m_send(k, p).start()
        m_got[r] = m_mine[r]

    @pl.loop(0, n_full)
    def _(n):
        off = pl.multiple_of(n * CHUNK, CHUNK)
        with jax.named_scope("ph_wait_v"):
            fetch(off, CHUNK, n % 2).wait()
        ladder(off, CHUNK, n, vbuf.at[n % 2])

        @pl.when(n + 2 < n_full)
        def _():
            fetch(pl.multiple_of((n + 2) * CHUNK, CHUNK), CHUNK, n % 2).start()

        @pl.when(n + P_AHEAD < n_full)
        def _():
            later = pl.multiple_of((n + P_AHEAD) * CHUNK, CHUNK)
            for k, p in enumerate(col_peers):
                p_send(later, CHUNK, n + P_AHEAD, k, p).start()

        @pl.when(n + P_AHEAD == n_full)
        def _():
            for k, p in enumerate(col_peers):
                p_send(n_full * CHUNK, LANES, n_full, k, p).start()

        @pl.when(n == 2)
        def _():
            with jax.named_scope("ph_form_x"):
                form_x()

        @pl.when(n == 5)
        def _():
            with jax.named_scope("ph_form_m"):
                form_m()

        @pl.when(n == 7)
        def _():
            with jax.named_scope("ph_form_d"):
                form_d()

        @pl.when(n >= 1)
        def _():
            across(pl.multiple_of((n - 1) * CHUNK, CHUNK), CHUNK, n - 1)

    ladder(n_full * CHUNK, LANES, n_full, vlast)
    across((n_full - 1) * CHUNK, CHUNK, n_full - 1)
    across(n_full * CHUNK, LANES, n_full)

    for k, p in enumerate(row_peers):
        m_send(k, p).wait_recv()
    for k, p in enumerate(col_peers):
        d_send(k, p).wait_recv()
    own_d.wait()
    ld_den.wait()

    def finish(off, width, n):
        at = pl.ds(off, width)
        hole_term = None
        for k in range(n_row):
            term = lax.dot_general(
                m_got[k], tcols[k, :, at], (((0,), (0,)), ((), ())), preferred_element_type=F32)
            hole_term = term if hole_term is None else hole_term + term
        own = part[r, :, at] + half[x, :, at] + xgot[:, at]
        for jh in range(n_col):
            v = own[jh * n_pair:(jh + 1) * n_pair] + got_d[jh, :, at]
            for i in range(occ):
                lo = i * n_occ + jh * occ
                xgot[lo:lo + occ, at] = v[i * occ:(i + 1) * occ]
        total = oovv[:, at].astype(F32) + xgot[:, at] + hole_term
        t32[:, at] = total / t32[:, at]

    @pl.loop(0, n_full)
    def _(n):
        off = pl.multiple_of(n * CHUNK, CHUNK)
        x_pass(off, CHUNK, n).wait_recv()
        finish(off, CHUNK, n)

    x_pass(n_full * CHUNK, LANES, n_full).wait_recv()
    finish(n_full * CHUNK, tail, n_full)
    st = pltpu.make_async_copy(t32, out_hbm, in_sem.at[8])
    st.start()

    for q in range(NQ):
        send_y(q).wait_send()
        send_z(q).wait_send()
        send_dz(q).wait_send()
        send_row(q).wait_send()
        send_lx(q).wait_send()
    row_p.wait_send()
    row_o.wait_send()
    for k, p in enumerate(row_peers):
        m_send(k, p).wait_send()
    for k, p in enumerate(col_peers):
        x_send(k, p).wait_send()
        d_send(k, p).wait_send()
    for n, (off, width) in enumerate(chunks):
        for k, p in enumerate(col_peers):
            p_send(off, width, n, k, p).wait_send()
        for w in range(2):
            h_send(off, width, n, w).wait_send()
        x_pass(off, width, n).wait_send()
    st.wait()


def solution(mesh):
    n_row = mesh.shape["row"]
    n_col = mesh.shape["col"]
    amp_spec = P("row", "col")
    wide_spec = P(None, "col")

    def local_sweep(t_blk, d_blk, oovv_blk, vvvv_blk, oooo_full, wd_blk, wx_blk):
        rows_dev, cols_dev = t_blk.shape
        n_occ = math.isqrt(oooo_full.shape[0])
        n_virt = wd_blk.shape[0] // n_occ
        occ, vir = n_occ // n_row, n_virt // n_col
        n_pair = occ * occ
        n_chunk = cols_dev // CHUNK + 1
        wide = -(-cols_dev // LANES) * LANES
        kc, jb = wd_blk.shape
        perm = np.eye(rows_dev, dtype=BF16).reshape(occ, n_col, occ, rows_dev).transpose(1, 0, 2, 3).reshape(rows_dev, rows_dev)
        n_sq = n_occ * n_occ
        swap = np.eye(n_sq, dtype=BF16).reshape(n_occ, n_occ, n_sq).transpose(1, 0, 2).reshape(n_sq, n_sq)
        dma = pltpu.SemaphoreType.DMA
        vm = pltpu.VMEM
        hbm = pl.BlockSpec(memory_space=pl.ANY)
        block = (rows_dev, cols_dev)
        return pl.pallas_call(
            functools.partial(sweep_kernel, (n_occ, n_virt, n_row, n_col)),
            out_shape=jax.ShapeDtypeStruct(block, F32),
            grid=(1,),
            in_specs=[hbm] * 4 + [pl.BlockSpec((cols_dev, LANES), lambda i: (0, cols_dev // LANES), pipeline_mode=pl.Buffered(1))] + [hbm] * 5,
            out_specs=hbm,
            scratch_shapes=[
                vm(block, F32), vm((n_col,) + block, BF16), vm((n_row,) + block, BF16), vm((n_row,) + block, BF16),
                vm((kc, jb), BF16), vm((jb, kc), BF16), vm((jb, kc), BF16),
                vm((kc, n_virt), BF16), vm((n_virt, kc), BF16), vm((n_virt, jb), F32), vm((jb, n_virt), F32),
                vm((n_pair, n_virt, n_virt), F32), vm((n_pair, n_virt, n_virt), F32),
                vm((n_col, n_pair, wide), F32), vm((n_col, n_pair, wide), F32),
                vm((n_col, n_pair, wide), F32), vm((n_col, n_pair, wide), F32),
                vm((n_row, rows_dev, wide), F32), vm((2, rows_dev, wide), F32),
                vm((rows_dev, wide), F32), vm((rows_dev, wide), F32),
                vm((2, cols_dev, CHUNK), BF16), vm(block, BF16), vm(oooo_full.shape, BF16),
                vm((rows_dev, rows_dev), BF16), vm((n_sq, n_sq), BF16),
                vm((rows_dev, n_sq), F32), vm((n_col, rows_dev, n_sq), F32),
                vm((n_row, rows_dev, rows_dev), BF16), vm((n_row, rows_dev, rows_dev), BF16),
                dma((10,)), dma((2,)), dma((2,)), dma((3, NQ)), dma((3, NQ)), dma((3, NQ)), dma((4, NQ)), dma((2, 4)),
                dma((2, NQ)), dma((3, n_chunk)), dma((3, n_chunk)), dma((2, 3)), dma((2, n_chunk)), dma((2, n_chunk)),
                dma((n_chunk,)), dma((n_chunk,)), dma((2, 3)), dma((2, 3)),
            ],
            compiler_params=pltpu.CompilerParams(
                collective_id=0, has_side_effects=True, vmem_limit_bytes=67043328),
        )(t_blk, d_blk, oovv_blk, vvvv_blk, vvvv_blk, oooo_full, wd_blk.T, wx_blk.T, jnp.asarray(perm), jnp.asarray(swap))

    return jax.shard_map(
        local_sweep, mesh=mesh,
        in_specs=(amp_spec, amp_spec, amp_spec, amp_spec, P(), wide_spec, wide_spec),
        out_specs=amp_spec, check_vma=False)
```

time: 128 us -> 88.9 us (0.69)
  Pallas kernels: 114 us -> 86.2 us
  local copies, waits for them, and re-layouts: 12.6 us -> 2.48 us
  other arithmetic: 1.45 us -> 0 us
    pallas_call x1, Pallas kernels: 114 us -> 86.2 us  [local_sweep(): pl.pallas_call(functools.partial(sweep_kernel, (n_occ, n_virt, n_row, n_c...]
    unnamed x5 -> x1, local copies, waits for them, and re-layouts: 9.94 us -> 2.48 us
    slice x1 -> x0, local copies, waits for them, and re-layouts: 2.47 us -> none  [local_sweep(): v_last = vvvv_blk[:, cols_dev // CHUNK * CHUNK:]]
    convert_element_type x2 -> x0, other arithmetic: 1.44 us -> none  [the longest x1 0.76 us: local_sweep(): jnp.eye(n_sq, dtype=BF16).reshape(n_occ, n_occ, n_sq).transpose(1, 0, 2)]
where the time goes in v2:
time: 88.9 us; the launch traced here: 88.7 us
  Pallas kernels  86.2 us (97%)
  local copies, waits for them, and re-layouts  2.48 us (3%)
    pallas_call x1, Pallas kernels, local_sweep(): pl.pallas_call(functools.partial(sweep_kernel, (n_occ, n_virt, n_row, n_c...  86.2 us
    unnamed x1, local copies, waits for them, and re-layouts  2.48 us

profile of v2, /device:TPU:0, one launch (start us, length us, event | category | flops | bytes accessed | tf_op | source)
XLA Modules:
  0.0 88.7 jit_solution(5911816217598170920)
XLA Ops:
  0.0 86.2 %shard_map.91 = f32[64,5184]{1,0:T(8,128)} custom-call(f32[64,5184]{1,0:T(8,128)} %t_hbm.1, f32[64,5184]{1,0:T(8,128)} %den_hbm.1, bf16[64,5184]{1,0:T(8,128)(2,1)} %oovv_hbm.1, bf16[5184,5184]{1,0:T(8,128)(2,1)} %vlast.1, bf16[5184,5184]{1,0:T(8,128)(2,1)} %vlast.1, bf16[256,256]{1,0:T(8,128)(2,1)} %oooo_hbm.1, bf16[576,2304]{1,0:T(8,128)(2,1)} %bitcast.2, ...), custom_call_target="tpu_custom_call" | custom-call | tf_op jit(solution)/shard_map/pallas_call | solution.py:479
  86.2 2.5 %copy.11 = f32[64,5184]{1,0:T(8,128)} copy(f32[64,5184]{1,0:T(8,128)} %shard_map.91) | data formatting | bytes 2654208

commit v3 on v2

--- a/solution.py
+++ b/solution.py
@@ -14,19 +14,19 @@
 MESH = pl.DeviceIdType.MESH
 CHUNK = 512
 LANES = 128
-P_AHEAD = 3
+D_FIRST, D_SECOND = 5, 7
+P_AHEAD = 6
 AHEAD = 2
 OVER_Y = 1
-FORWARD = ((2, (0,)), (3, (1,)), (4, (2, 3)))
 NQ = 4
 
 
 def sweep_kernel(
     dims,
     t_hbm, den_hbm, oovv_hbm, vvvv_hbm, vlast, oooo_hbm, wd_hbm, wx_hbm, perm_hbm, swap_hbm,
-    out_hbm,
+    out,
     t32, rows, lad, tcols, wd, wdt, wxt, tr, ta, r3, r5, sd, sp, msg_d, msg_p, got_d, got_p,
-    part, half, xsend, xgot, vbuf, oovv, oooo, perm, swap, xpart, xgot_part, m_mine, m_got,
+    part, half, xsend, xgot, turned, vbuf, oovv, oooo, perm, swap, xpart, xgot_part, m_mine, m_got,
     in_sem, vb_sem, loc_sem, ts_sem, tr_sem, ls_sem, lr_sem, g_sem,
     rx_sem, ps_sem, pr_sem, d_sem, hs_sem, hr_sem, xs_sem, xr_sem, x_sem, m_sem,
 ):
@@ -159,17 +159,18 @@
                 a = ab * n_occ + t
                 lo = (a % vir) * n_virt
                 stack.append(rows[a // vir, lines, lo:lo + n_virt])
-            turned = jnp.dot(swap[...], jnp.concatenate(stack, axis=0), preferred_element_type=F32).astype(BF16)
+            lines_k = jnp.dot(swap[...], jnp.concatenate(stack, axis=0), preferred_element_type=F32).astype(BF16)
             for k in range(n_occ):
-                line = turned[k * n_occ:(k + 1) * n_occ]
+                line = lines_k[k * n_occ:(k + 1) * n_occ]
                 tr[k * n_virt + ab * n_occ:k * n_virt + (ab + 1) * n_occ, :] = line
                 ta[ab * n_occ:(ab + 1) * n_occ, k * n_virt:(k + 1) * n_virt] = line
 
-    def particle_hole(i):
+    def particle_hole(i, between):
         with jax.named_scope("ph_spread"):
             spread(i)
         with jax.named_scope("ph_r5"):
             r5[...] = jnp.dot(wxt[...], tr[...], preferred_element_type=F32)
+        between()
         with jax.named_scope("ph_r3"):
             r3[...] = jnp.dot(ta[...], wd[...], preferred_element_type=F32)
         with jax.named_scope("ph_diff"):
@@ -178,25 +179,22 @@
                 sd[i * occ + j] = diff
                 sp[j * occ + i] = diff.T
 
-    @pl.loop(0, NQ + 1)
-    def _(q):
-        @pl.when(q < NQ)
-        def _():
-            send_z(q).wait_recv()
-
-            @pl.when(jnp.logical_not(own_ladder))
-            def _():
-                send_lx(q).start()
-
-            send_y(q).wait_recv()
-
-            @pl.when(q == OVER_Y)
-            def _():
-                send_dy(q).start()
-
-            @pl.when(q != OVER_Y)
-            def _():
-                send_dz(q).start()
+    def stage(q):
+        send_z(q).wait_recv()
+
+        @pl.when(jnp.logical_not(own_ladder))
+        def _():
+            send_lx(q).start()
+
+        send_y(q).wait_recv()
+
+        @pl.when(q == OVER_Y)
+        def _():
+            send_dy(q).start()
+
+        @pl.when(q != OVER_Y)
+        def _():
+            send_dz(q).start()
 
         @pl.when(q + AHEAD < NQ)
         def _():
@@ -207,20 +205,36 @@
             def _():
                 send_lx(q + AHEAD).start()
 
-        @pl.when(q + 1 < NQ)
-        def _():
-            send_row(q + 1).start()
-
-        for at, pieces in FORWARD:
-            @pl.when(q == at)
+    def on_step(q, step, act, *args):
+        @pl.when(q == step)
+        def _():
+            act(*args)
+
+    def go_row(q):
+        send_row(q).start()
+
+    with jax.named_scope("ph_stages"):
+        stage(0)
+        stage(1)
+        go_row(1)
+
+    @pl.loop(0, NQ)
+    def _(q):
+        send_dz(q).wait_recv()
+        on_step(q, 0, go_row, 2)
+        on_step(q, 1, forward_ladder, 0)
+        on_step(q, 3, forward_ladder, 3)
+
+        def between():
+            @pl.when(q + 2 < NQ)
             def _():
-                for w in pieces:
-                    forward_ladder(w)
-
-        @pl.when(q >= 1)
-        def _():
-            send_dz(q - 1).wait_recv()
-            particle_hole(q - 1)
+                stage(q + 2)
+
+            on_step(q, 1, forward_ladder, 1)
+            on_step(q, 2, forward_ladder, 2)
+            on_step(q, 2, go_row, 3)
+
+        particle_hole(q, between)
 
     lad_p = remote(rows.at[r_p], lad.at[r], g_sem.at[0, 3], g_sem.at[1, 3], r_p, c)
     lad_p.start()
@@ -249,10 +263,18 @@
     own_p = pltpu.make_async_copy(msg_p.at[c], got_p.at[c], loc_sem.at[0])
     own_p.start()
 
-    def d_send(k, p):
-        return remote(msg_d.at[p], got_d.at[c], d_sem.at[0, k], d_sem.at[1, k], r, p)
+    d_cut = n_full // 2 * CHUNK
+    d_halves = ((0, d_cut), (d_cut, msg_d.shape[2] - d_cut))
+
+    def d_send(w, k, p):
+        at = pl.ds(*d_halves[w])
+        return remote(msg_d.at[p, :, at], got_d.at[c, :, at], d_sem.at[0, w, k], d_sem.at[1, w, k], r, p)
 
     own_d = pltpu.make_async_copy(msg_d.at[c], got_d.at[c], loc_sem.at[1])
+
+    def go_d(w):
+        for k, p in enumerate(col_peers):
+            d_send(w, k, p).start()
 
     def form_d():
         @pl.loop(0, n_col)
@@ -260,8 +282,7 @@
             for a in range(vir):
                 msg_d[k, :, a * n_virt:(a + 1) * n_virt] = sd[:, k * vir + a, :]
 
-        for k, p in enumerate(col_peers):
-            d_send(k, p).start()
+        go_d(0)
         own_d.start()
 
     lad_p.wait_recv()
@@ -298,15 +319,14 @@
         return remote(part.at[2 * w + 1 - u, :, at], half.at[w, :, at], hs_sem.at[w, n], hr_sem.at[w, n], r_p, c)
 
     def x_pass(off, width, n):
-        at = pl.ds(off, width)
-        return remote(xsend.at[:, at], xgot.at[:, at], xs_sem.at[n], xr_sem.at[n], r_s, c)
+        return remote(xsend.at[n, :, pl.ds(0, width)], xgot.at[n, :, pl.ds(0, width)], xs_sem.at[n], xr_sem.at[n], r_s, c)
 
     def across(off, width, n):
         at = pl.ds(off, width)
         with jax.named_scope("ph_wait_h"):
             for w in range(2):
                 h_send(off, width, n, w).wait_recv()
-        xsend[:, at] = part[2 * (1 - x) + u, :, at] + half[1 - x, :, at]
+        xsend[n, :, 0:width] = part[2 * (1 - x) + u, :, at] + half[1 - x, :, at]
         x_pass(off, width, n).start()
 
     def ladder(off, width, n, v_ref):
@@ -380,15 +400,19 @@
             with jax.named_scope("ph_form_x"):
                 form_x()
 
-        @pl.when(n == 5)
+        @pl.when(n == 8)
         def _():
             with jax.named_scope("ph_form_m"):
                 form_m()
 
-        @pl.when(n == 7)
+        @pl.when(n == D_FIRST)
         def _():
             with jax.named_scope("ph_form_d"):
                 form_d()
+
+        @pl.when(n == D_SECOND)
+        def _():
+            go_d(1)
 
         @pl.when(n >= 1)
         def _():
@@ -398,39 +422,61 @@
     across((n_full - 1) * CHUNK, CHUNK, n_full - 1)
     across(n_full * CHUNK, LANES, n_full)
 
-    for k, p in enumerate(row_peers):
-        m_send(k, p).wait_recv()
-    for k, p in enumerate(col_peers):
-        d_send(k, p).wait_recv()
-    own_d.wait()
+    with jax.named_scope("ph_fin_m"):
+        for k, p in enumerate(row_peers):
+            m_send(k, p).wait_recv()
     ld_den.wait()
 
-    def finish(off, width, n):
+    def hole_term(off, width):
         at = pl.ds(off, width)
-        hole_term = None
+        total = None
         for k in range(n_row):
             term = lax.dot_general(
                 m_got[k], tcols[k, :, at], (((0,), (0,)), ((), ())), preferred_element_type=F32)
-            hole_term = term if hole_term is None else hole_term + term
-        own = part[r, :, at] + half[x, :, at] + xgot[:, at]
+            total = term if total is None else total + term
+        part[r_s, :, at] = total + oovv[:, at].astype(F32)
+        part[r, :, pl.ds(off, width)] += half[x, :, at]
+
+    def finish(off, width, n):
+        at = pl.ds(off, width)
+        own = part[r, :, at] + xgot[n, :, 0:width]
         for jh in range(n_col):
             v = own[jh * n_pair:(jh + 1) * n_pair] + got_d[jh, :, at]
             for i in range(occ):
                 lo = i * n_occ + jh * occ
-                xgot[lo:lo + occ, at] = v[i * occ:(i + 1) * occ]
-        total = oovv[:, at].astype(F32) + xgot[:, at] + hole_term
-        t32[:, at] = total / t32[:, at]
+                turned[lo:lo + occ, 0:width] = v[i * occ:(i + 1) * occ]
+        out[:, at] = (part[r_s, :, at] + turned[:, 0:width]) / t32[:, at]
+
+    def full(n):
+        return pl.multiple_of(n * CHUNK, CHUNK)
 
     @pl.loop(0, n_full)
     def _(n):
-        off = pl.multiple_of(n * CHUNK, CHUNK)
-        x_pass(off, CHUNK, n).wait_recv()
-        finish(off, CHUNK, n)
+        hole_term(full(n), CHUNK)
+
+    hole_term(n_full * CHUNK, tail)
+    n_cut = d_cut // CHUNK
+
+    def wait_d(w):
+        with jax.named_scope("ph_fin_d"):
+            for k, p in enumerate(col_peers):
+                d_send(w, k, p).wait_recv()
+
+    own_d.wait()
+    wait_d(0)
+
+    @pl.loop(0, n_full)
+    def _(n):
+        @pl.when(n == n_cut)
+        def _():
+            wait_d(1)
+
+        with jax.named_scope("ph_fin_x"):
+            x_pass(full(n), CHUNK, n).wait_recv()
+        finish(full(n), CHUNK, n)
 
     x_pass(n_full * CHUNK, LANES, n_full).wait_recv()
     finish(n_full * CHUNK, tail, n_full)
-    st = pltpu.make_async_copy(t32, out_hbm, in_sem.at[8])
-    st.start()
 
     for q in range(NQ):
         send_y(q).wait_send()
@@ -444,14 +490,14 @@
         m_send(k, p).wait_send()
     for k, p in enumerate(col_peers):
         x_send(k, p).wait_send()
-        d_send(k, p).wait_send()
+        for w in range(2):
+            d_send(w, k, p).wait_send()
     for n, (off, width) in enumerate(chunks):
         for k, p in enumerate(col_peers):
             p_send(off, width, n, k, p).wait_send()
         for w in range(2):
             h_send(off, width, n, w).wait_send()
         x_pass(off, width, n).wait_send()
-    st.wait()
 
 
 def solution(mesh):
@@ -478,10 +524,10 @@
         block = (rows_dev, cols_dev)
         return pl.pallas_call(
             functools.partial(sweep_kernel, (n_occ, n_virt, n_row, n_col)),
-            out_shape=jax.ShapeDtypeStruct(block, F32),
+            out_shape=pltpu.VMEM(block, F32),
             grid=(1,),
             in_specs=[hbm] * 4 + [pl.BlockSpec((cols_dev, LANES), lambda i: (0, cols_dev // LANES), pipeline_mode=pl.Buffered(1))] + [hbm] * 5,
-            out_specs=hbm,
+            out_specs=pl.BlockSpec(memory_space=pltpu.VMEM),
             scratch_shapes=[
                 vm(block, F32), vm((n_col,) + block, BF16), vm((n_row,) + block, BF16), vm((n_row,) + block, BF16),
                 vm((kc, jb), BF16), vm((jb, kc), BF16), vm((jb, kc), BF16),
@@ -490,17 +536,17 @@
                 vm((n_col, n_pair, wide), F32), vm((n_col, n_pair, wide), F32),
                 vm((n_col, n_pair, wide), F32), vm((n_col, n_pair, wide), F32),
                 vm((n_row, rows_dev, wide), F32), vm((2, rows_dev, wide), F32),
-                vm((rows_dev, wide), F32), vm((rows_dev, wide), F32),
+                vm((n_chunk, rows_dev, CHUNK), F32), vm((n_chunk, rows_dev, CHUNK), F32), vm((rows_dev, CHUNK), F32),
                 vm((2, cols_dev, CHUNK), BF16), vm(block, BF16), vm(oooo_full.shape, BF16),
                 vm((rows_dev, rows_dev), BF16), vm((n_sq, n_sq), BF16),
                 vm((rows_dev, n_sq), F32), vm((n_col, rows_dev, n_sq), F32),
                 vm((n_row, rows_dev, rows_dev), BF16), vm((n_row, rows_dev, rows_dev), BF16),
-                dma((10,)), dma((2,)), dma((2,)), dma((3, NQ)), dma((3, NQ)), dma((3, NQ)), dma((4, NQ)), dma((2, 4)),
-                dma((2, NQ)), dma((3, n_chunk)), dma((3, n_chunk)), dma((2, 3)), dma((2, n_chunk)), dma((2, n_chunk)),
+                dma((10,)), dma((2,)), dma((2,)), dma((3, NQ)), dma((3, NQ)), dma((4, NQ)), dma((4, NQ)), dma((2, 4)),
+                dma((2, NQ)), dma((3, n_chunk)), dma((3, n_chunk)), dma((2, 2, 3)), dma((2, n_chunk)), dma((2, n_chunk)),
                 dma((n_chunk,)), dma((n_chunk,)), dma((2, 3)), dma((2, 3)),
             ],
             compiler_params=pltpu.CompilerParams(
-                collective_id=0, has_side_effects=True, vmem_limit_bytes=67043328),
+                collective_id=0, has_side_effects=True, vmem_limit_bytes=65536000),
         )(t_blk, d_blk, oovv_blk, vvvv_blk, vvvv_blk, oooo_full, wd_blk.T, wx_blk.T, jnp.asarray(perm), jnp.asarray(swap))
 
     return jax.shard_map(

time: 88.9 us -> 83 us (0.934)
  Pallas kernels: 86.2 us -> 81.7 us
  local copies, waits for them, and re-layouts: 2.48 us -> 1.07 us
    pallas_call x1, Pallas kernels: 86.2 us -> 81.7 us  [local_sweep(): pl.pallas_call(functools.partial(sweep_kernel, (n_occ, n_virt, n_row, n_c...]
    unnamed x1, local copies, waits for them, and re-layouts: 2.48 us -> 1.07 us
where the time goes in v3:
time: 83 us; the launch traced here: 82.7 us
  Pallas kernels  81.7 us (98%)
  local copies, waits for them, and re-layouts  1.07 us (1%)
    pallas_call x1, Pallas kernels, local_sweep(): pl.pallas_call(functools.partial(sweep_kernel, (n_occ, n_virt, n_row, n_c...  81.7 us

profile of v3, /device:TPU:0, one launch (start us, length us, event | category | flops | bytes accessed | tf_op | source)
XLA Modules:
  0.0 82.7 jit_solution(13022922165420549555)
XLA Ops:
  0.0 81.7 %shard_map.91 = f32[64,5184]{1,0:T(8,128)S(1)} custom-call(f32[64,5184]{1,0:T(8,128)} %t_hbm.1, f32[64,5184]{1,0:T(8,128)} %den_hbm.1, bf16[64,5184]{1,0:T(8,128)(2,1)} %oovv_hbm.1, bf16[5184,5184]{1,0:T(8,128)(2,1)} %vlast.1, bf16[5184,5184]{1,0:T(8,128)(2,1)} %vlast.1, bf16[256,256]{1,0:T(8,128)(2,1)} %oooo_hbm.1, bf16[576,2304]{1,0:T(8,128)(2,1)} %bitcast.2, ...), custom_call_target="tpu_custom_call" | custom-call | tf_op jit(solution)/shard_map/pallas_call | solution.py:525
  81.7 1.1 %copy.11 = f32[64,5184]{1,0:T(8,128)} copy(f32[64,5184]{1,0:T(8,128)S(1)} %shard_map.91) | data formatting | bytes 2654208

commit v4 on v3

--- a/solution.py
+++ b/solution.py
@@ -15,7 +15,7 @@
 CHUNK = 512
 LANES = 128
 D_FIRST, D_SECOND = 5, 7
-P_AHEAD = 6
+P_FIRST, P_AHEAD = 2, 6
 AHEAD = 2
 OVER_Y = 1
 NQ = 4
@@ -106,6 +106,13 @@
         k = 2 * (1 - x) + w
         return remote(piece(lad, k, q), piece(lad, k, q), ls_sem.at[1 + w, q], lr_sem.at[2 + w, q], r, c_y)
 
+    def send_lo(q):
+        k = 2 * (1 - x) + 1 - y
+        return remote(piece(rows, k, q), piece(lad, r, q), ls_sem.at[3, q], lr_sem.at[2 + u, q], k, c)
+
+    def go_lo(q):
+        send_lo(q).start()
+
     own_ladder = z == 1 - x
     direct = u == y
 
@@ -170,15 +177,16 @@
             spread(i)
         with jax.named_scope("ph_r5"):
             r5[...] = jnp.dot(wxt[...], tr[...], preferred_element_type=F32)
+            r3[...] = jnp.dot(ta[...], wd[...], preferred_element_type=F32)
         between()
-        with jax.named_scope("ph_r3"):
-            r3[...] = jnp.dot(ta[...], wd[...], preferred_element_type=F32)
         with jax.named_scope("ph_diff"):
             for j in range(occ):
                 diff = r3[:, j * n_virt:(j + 1) * n_virt] - r5[j * n_virt:(j + 1) * n_virt, :]
                 sd[i * occ + j] = diff
                 sp[j * occ + i] = diff.T
 
+    lad_p = remote(rows.at[r_p], lad.at[r], g_sem.at[0, 3], g_sem.at[1, 3], r_p, c)
+
     def stage(q):
         send_z(q).wait_recv()
 
@@ -216,14 +224,17 @@
     with jax.named_scope("ph_stages"):
         stage(0)
         stage(1)
-        go_row(1)
 
     @pl.loop(0, NQ)
     def _(q):
+        on_step(q, 2, forward_ladder, 2)
         send_dz(q).wait_recv()
-        on_step(q, 0, go_row, 2)
-        on_step(q, 1, forward_ladder, 0)
-        on_step(q, 3, forward_ladder, 3)
+
+        @pl.when(q == NQ - 1)
+        def _():
+            lad_p.start()
+
+        on_step(q, 0, go_lo, 0)
 
         def between():
             @pl.when(q + 2 < NQ)
@@ -231,14 +242,12 @@
                 stage(q + 2)
 
             on_step(q, 1, forward_ladder, 1)
-            on_step(q, 2, forward_ladder, 2)
-            on_step(q, 2, go_row, 3)
+            on_step(q, 1, go_row, 1)
+            on_step(q, 2, forward_ladder, 3)
+            on_step(q, 2, go_row, 2)
+            on_step(q, 3, go_row, 3)
 
         particle_hole(q, between)
-
-    lad_p = remote(rows.at[r_p], lad.at[r], g_sem.at[0, 3], g_sem.at[1, 3], r_p, c)
-    lad_p.start()
-    lad[r] = rows[r]
 
     n_pair = occ * occ
     pad = pl.ds(cols_dev - tail, LANES)
@@ -257,9 +266,12 @@
         return remote(msg_p.at[p, :, at], got_p.at[c, :, at], ps_sem.at[k, n], pr_sem.at[k, n], r, p)
 
     chunks = [(n * CHUNK, CHUNK) for n in range(n_full)] + [(n_full * CHUNK, LANES)]
-    for n, (off, width) in enumerate(chunks[:P_AHEAD]):
-        for k, p in enumerate(col_peers):
-            p_send(off, width, n, k, p).start()
+    def go_p(first, last):
+        for n, (off, width) in enumerate(chunks[first:last], first):
+            for k, p in enumerate(col_peers):
+                p_send(off, width, n, k, p).start()
+
+    go_p(0, P_FIRST)
     own_p = pltpu.make_async_copy(msg_p.at[c], got_p.at[c], loc_sem.at[0])
     own_p.start()
 
@@ -285,7 +297,17 @@
         go_d(0)
         own_d.start()
 
+    ld_perm.wait()
+
+    def permute(k, src):
+        for off in range(0, cols_dev, CHUNK):
+            width = min(CHUNK, cols_dev - off)
+            block = jnp.dot(perm[...], src[:, off:off + width], preferred_element_type=F32)
+            lad[k, :, off:off + width] = block.astype(BF16)
+
+    permute(r, rows.at[r])
     lad_p.wait_recv()
+    permute(r_p, lad.at[r_p])
 
     @pl.when(jnp.logical_not(direct))
     def _():
@@ -295,18 +317,17 @@
 
     @pl.when(direct)
     def _():
-        for q in range(NQ):
+        for w in range(2):
+            recv_lx(w, 0).wait_recv()
+        for q in range(1, NQ):
             for w in range(2):
                 send_ly(w, q).wait_send()
-    lad_p.wait_send()
-    ld_perm.wait()
-
-    @pl.loop(0, n_row)
-    def _(k):
-        for off in range(0, cols_dev, CHUNK):
-            width = min(CHUNK, cols_dev - off)
-            block = jnp.dot(perm[...], lad[k, :, off:off + width], preferred_element_type=F32)
-            lad[k, :, off:off + width] = block.astype(BF16)
+
+    go_p(P_FIRST, P_AHEAD)
+
+    @pl.loop(0, 2)
+    def _(w):
+        permute(2 * (1 - x) + w, lad.at[2 * (1 - x) + w])
 
     own_p.wait()
 
@@ -400,7 +421,7 @@
             with jax.named_scope("ph_form_x"):
                 form_x()
 
-        @pl.when(n == 8)
+        @pl.when(n == 6)
         def _():
             with jax.named_scope("ph_form_m"):
                 form_m()
@@ -414,7 +435,11 @@
         def _():
             go_d(1)
 
-        @pl.when(n >= 1)
+        @pl.when(n == 0)
+        def _():
+            across(0, CHUNK, 0)
+
+        @pl.when(n >= 2)
         def _():
             across(pl.multiple_of((n - 1) * CHUNK, CHUNK), CHUNK, n - 1)
 
@@ -478,6 +503,8 @@
     x_pass(n_full * CHUNK, LANES, n_full).wait_recv()
     finish(n_full * CHUNK, tail, n_full)
 
+    lad_p.wait_send()
+    send_lo(0).wait_send()
     for q in range(NQ):
         send_y(q).wait_send()
         send_z(q).wait_send()

time: 83 us -> 80.5 us (0.970)
  Pallas kernels: 81.7 us -> 79.1 us
    pallas_call x1, Pallas kernels: 81.7 us -> 79.1 us  [local_sweep(): pl.pallas_call(functools.partial(sweep_kernel, (n_occ, n_virt, n_row, n_c...]
where the time goes in v4:
time: 80.5 us; the launch traced here: 80.2 us
  Pallas kernels  79.1 us (98%)
  local copies, waits for them, and re-layouts  1.07 us (1%)
    pallas_call x1, Pallas kernels, local_sweep(): pl.pallas_call(functools.partial(sweep_kernel, (n_occ, n_virt, n_row, n_c...  79.1 us

profile of v4, /device:TPU:0, one launch (start us, length us, event | category | flops | bytes accessed | tf_op | source)
XLA Modules:
  0.0 80.2 jit_solution(5909103024043392787)
XLA Ops:
  0.0 79.1 %shard_map.91 = f32[64,5184]{1,0:T(8,128)S(1)} custom-call(f32[64,5184]{1,0:T(8,128)} %t_hbm.1, f32[64,5184]{1,0:T(8,128)} %den_hbm.1, bf16[64,5184]{1,0:T(8,128)(2,1)} %oovv_hbm.1, bf16[5184,5184]{1,0:T(8,128)(2,1)} %vlast.1, bf16[5184,5184]{1,0:T(8,128)(2,1)} %vlast.1, bf16[256,256]{1,0:T(8,128)(2,1)} %oooo_hbm.1, bf16[576,2304]{1,0:T(8,128)(2,1)} %bitcast.2, ...), custom_call_target="tpu_custom_call" | custom-call | tf_op jit(solution)/shard_map/pallas_call | solution.py:552
  79.1 1.1 %copy.11 = f32[64,5184]{1,0:T(8,128)} copy(f32[64,5184]{1,0:T(8,128)S(1)} %shard_map.91) | data formatting | bytes 2654208

commit v5 on v4

--- a/solution.py
+++ b/solution.py
@@ -12,9 +12,13 @@
 F32 = jnp.float32
 BF16 = jnp.bfloat16
 MESH = pl.DeviceIdType.MESH
-CHUNK = 512
+CHUNK = 256
+WIDE = 512
+RING = 4
+DEPTH = 4
 LANES = 128
-D_FIRST, D_SECOND = 5, 7
+X_STEP, M_STEP = 6, 14
+D_FIRST, D_SECOND = 9, 13
 P_FIRST, P_AHEAD = 2, 6
 AHEAD = 2
 OVER_Y = 1
@@ -23,11 +27,11 @@
 
 def sweep_kernel(
     dims,
-    t_hbm, den_hbm, oovv_hbm, vvvv_hbm, vlast, oooo_hbm, wd_hbm, wx_hbm, perm_hbm, swap_hbm,
+    t_hbm, den_hbm, oovv_hbm, vvvv_hbm, oooo_hbm, wd_hbm, wx_hbm, perm_hbm, swap_hbm,
     out,
     t32, rows, lad, tcols, wd, wdt, wxt, tr, ta, r3, r5, sd, sp, msg_d, msg_p, got_d, got_p,
-    part, half, xsend, xgot, turned, vbuf, oovv, oooo, perm, swap, xpart, xgot_part, m_mine, m_got,
-    in_sem, vb_sem, loc_sem, ts_sem, tr_sem, ls_sem, lr_sem, g_sem,
+    part, half, xsend, xgot, turned, vbuf, vlast, oovv, oooo, perm, swap, xpart, xgot_part, m_mine, m_got,
+    in_sem, vb_sem, loc_sem, ts_sem, tr_sem, ls_sem, lr_sem, ly_sem, g_sem,
     rx_sem, ps_sem, pr_sem, d_sem, hs_sem, hr_sem, xs_sem, xr_sem, x_sem, m_sem,
 ):
     n_occ, n_virt, n_row, n_col = dims
@@ -68,9 +72,11 @@
     def fetch(off, width, slot):
         return pltpu.make_async_copy(vvvv_hbm.at[:, pl.ds(off, width)], vbuf.at[slot], vb_sem.at[slot])
 
-    for s in range(2):
+    for s in range(DEPTH):
         fetch(s * CHUNK, CHUNK, s).start()
 
+    ld_last = load(vvvv_hbm.at[:, pl.ds(n_full * CHUNK, tail)], vlast, 8)
+    ld_last.start()
     barrier = pltpu.get_barrier_semaphore()
     for p in col_peers:
         pl.semaphore_signal(barrier, inc=1, device_id={"row": r, "col": p}, device_id_type=MESH)
@@ -82,33 +88,33 @@
         return ref.at[k, pl.ds(pl.multiple_of(q * qrows, qrows), qrows), :]
 
     def send_y(q):
-        return remote(piece(rows, c, q), piece(rows, c, q), ts_sem.at[0, q], tr_sem.at[0, q], r, c_y)
+        return remote(piece(rows, c, q), piece(rows, c, q), ts_sem.at[0], tr_sem.at[0, q], r, c_y)
 
     def send_z(q):
-        return remote(piece(rows, c, q), piece(rows, c, q), ts_sem.at[1, q], tr_sem.at[1, q], r, c_z)
+        return remote(piece(rows, c, q), piece(rows, c, q), ts_sem.at[1], tr_sem.at[1, q], r, c_z)
 
     def send_dz(q):
-        return remote(piece(rows, c_y, q), piece(rows, c_y, q), ts_sem.at[2, q], tr_sem.at[2, q], r, c_z)
+        return remote(piece(rows, c_y, q), piece(rows, c_y, q), ts_sem.at[2], tr_sem.at[2, q], r, c_z)
 
     def send_dy(q):
-        return remote(piece(rows, c_z, q), piece(rows, c_z, q), ts_sem.at[2, q], tr_sem.at[2, q], r, c_y)
+        return remote(piece(rows, c_z, q), piece(rows, c_z, q), ts_sem.at[2], tr_sem.at[2, q], r, c_y)
 
     blk_x = 2 * (1 - x) + y
 
     def send_lx(q):
-        return remote(piece(rows, blk_x, q), piece(lad, r, q), ls_sem.at[0, q], lr_sem.at[u, q], blk_x, c)
+        return remote(piece(rows, blk_x, q), piece(lad, r, q), ls_sem.at[0], lr_sem.at[u, q], blk_x, c)
 
     def recv_lx(w, q):
         k = 2 * (1 - x) + w
-        return remote(piece(lad, k, q), piece(lad, k, q), ls_sem.at[0, q], lr_sem.at[w, q], blk_x, c)
+        return remote(piece(lad, k, q), piece(lad, k, q), ls_sem.at[0], lr_sem.at[w, q], blk_x, c)
 
     def send_ly(w, q):
         k = 2 * (1 - x) + w
-        return remote(piece(lad, k, q), piece(lad, k, q), ls_sem.at[1 + w, q], lr_sem.at[2 + w, q], r, c_y)
+        return remote(piece(lad, k, q), piece(lad, k, q), ls_sem.at[1 + w], ly_sem.at[w], r, c_y)
 
     def send_lo(q):
         k = 2 * (1 - x) + 1 - y
-        return remote(piece(rows, k, q), piece(lad, r, q), ls_sem.at[3, q], lr_sem.at[2 + u, q], k, c)
+        return remote(piece(rows, k, q), piece(lad, r, q), ls_sem.at[3], ly_sem.at[u], k, c)
 
     def go_lo(q):
         send_lo(q).start()
@@ -130,7 +136,7 @@
     ld_den.start()
 
     def send_row(q):
-        return remote(piece(rows, c, q), piece(tcols, r, q), rx_sem.at[0, q], rx_sem.at[1, q], r_s, c)
+        return remote(piece(rows, c, q), piece(tcols, r, q), rx_sem.at[0], rx_sem.at[1], r_s, c)
 
     row_p = remote(rows.at[c], tcols.at[r], g_sem.at[0, 0], g_sem.at[1, 0], r_p, c)
     row_o = remote(tcols.at[r_s], tcols.at[r_s], g_sem.at[0, 1], g_sem.at[1, 1], r_p, c)
@@ -263,9 +269,10 @@
 
     def p_send(off, width, n, k, p):
         at = pl.ds(off, width)
-        return remote(msg_p.at[p, :, at], got_p.at[c, :, at], ps_sem.at[k, n], pr_sem.at[k, n], r, p)
-
-    chunks = [(n * CHUNK, CHUNK) for n in range(n_full)] + [(n_full * CHUNK, LANES)]
+        return remote(msg_p.at[p, :, at], got_p.at[c, :, at], ps_sem.at[k], pr_sem.at[k, n], r, p)
+
+    n_wide = cols_dev // WIDE
+    chunks = [(n * WIDE, WIDE) for n in range(n_wide)] + [(n_wide * WIDE, LANES)]
     def go_p(first, last):
         for n, (off, width) in enumerate(chunks[first:last], first):
             for k, p in enumerate(col_peers):
@@ -280,7 +287,7 @@
 
     def d_send(w, k, p):
         at = pl.ds(*d_halves[w])
-        return remote(msg_d.at[p, :, at], got_d.at[c, :, at], d_sem.at[0, w, k], d_sem.at[1, w, k], r, p)
+        return remote(msg_d.at[p, :, at], got_d.at[c, :, at], d_sem.at[0, k], d_sem.at[1 + w, k], r, p)
 
     own_d = pltpu.make_async_copy(msg_d.at[c], got_d.at[c], loc_sem.at[1])
 
@@ -300,8 +307,8 @@
     ld_perm.wait()
 
     def permute(k, src):
-        for off in range(0, cols_dev, CHUNK):
-            width = min(CHUNK, cols_dev - off)
+        for off in range(0, cols_dev, 4 * LANES):
+            width = min(4 * LANES, cols_dev - off)
             block = jnp.dot(perm[...], src[:, off:off + width], preferred_element_type=F32)
             lad[k, :, off:off + width] = block.astype(BF16)
 
@@ -311,17 +318,17 @@
 
     @pl.when(jnp.logical_not(direct))
     def _():
-        for q in range(NQ):
-            for w in range(2):
-                send_ly(w, q).wait_recv()
+        for w in range(2):
+            whole = lad.at[2 * (1 - x) + w]
+            remote(whole, whole, ls_sem.at[1 + w], ly_sem.at[w], r, c_y).wait_recv()
 
     @pl.when(direct)
     def _():
         for w in range(2):
             recv_lx(w, 0).wait_recv()
-        for q in range(1, NQ):
-            for w in range(2):
-                send_ly(w, q).wait_send()
+        for w in range(2):
+            rest = lad.at[2 * (1 - x) + w, pl.ds(qrows, rows_dev - qrows), :]
+            remote(rest, rest, ls_sem.at[1 + w], ly_sem.at[w], r, c_y).wait_send()
 
     go_p(P_FIRST, P_AHEAD)
 
@@ -331,16 +338,15 @@
 
     own_p.wait()
 
-    for q in range(NQ):
-        send_row(q).wait_recv()
+    remote(tcols.at[r_s], tcols.at[r_s], rx_sem.at[0], rx_sem.at[1], r_s, c).wait_recv()
     row_o.start()
 
     def h_send(off, width, n, w):
         at = pl.ds(off, width)
-        return remote(part.at[2 * w + 1 - u, :, at], half.at[w, :, at], hs_sem.at[w, n], hr_sem.at[w, n], r_p, c)
+        return remote(part.at[2 * w + 1 - u, :, at], half.at[w, :, at], hs_sem.at[w], hr_sem.at[w, n % RING], r_p, c)
 
     def x_pass(off, width, n):
-        return remote(xsend.at[n, :, pl.ds(0, width)], xgot.at[n, :, pl.ds(0, width)], xs_sem.at[n], xr_sem.at[n], r_s, c)
+        return remote(xsend.at[n, :, pl.ds(0, width)], xgot.at[n, :, pl.ds(0, width)], xs_sem.at[0], xr_sem.at[n], r_s, c)
 
     def across(off, width, n):
         at = pl.ds(off, width)
@@ -350,15 +356,13 @@
         xsend[n, :, 0:width] = part[2 * (1 - x) + u, :, at] + half[1 - x, :, at]
         x_pass(off, width, n).start()
 
-    def ladder(off, width, n, v_ref):
+    def ladder(off, width, n, v_ref, arrive):
         at = pl.ds(off, width)
         with jax.named_scope("ph_dot"):
             t_all = lad[...].reshape(n_row * rows_dev, cols_dev)
-            prod = jnp.dot(t_all, v_ref[:, 0:min(width, cols_dev - off) if width == LANES else width], preferred_element_type=F32)
+            prod = jnp.dot(t_all, v_ref[...], preferred_element_type=F32)
             part[:, :, pl.ds(off, prod.shape[1])] = prod.reshape(n_row, rows_dev, prod.shape[1])
-        with jax.named_scope("ph_wait_p"):
-            for k, p in enumerate(col_peers):
-                p_send(off, width, n, k, p).wait_recv()
+        arrive()
         mine = pl.ds(pl.multiple_of(r * n_pair, n_pair), n_pair)
         for k in range(n_col):
             part[k, mine, at] += got_p[k, :, at]
@@ -394,34 +398,45 @@
             m_send(k, p).start()
         m_got[r] = m_mine[r]
 
+    per = WIDE // CHUNK
+
     @pl.loop(0, n_full)
     def _(n):
         off = pl.multiple_of(n * CHUNK, CHUNK)
         with jax.named_scope("ph_wait_v"):
-            fetch(off, CHUNK, n % 2).wait()
-        ladder(off, CHUNK, n, vbuf.at[n % 2])
-
-        @pl.when(n + 2 < n_full)
-        def _():
-            fetch(pl.multiple_of((n + 2) * CHUNK, CHUNK), CHUNK, n % 2).start()
-
-        @pl.when(n + P_AHEAD < n_full)
-        def _():
-            later = pl.multiple_of((n + P_AHEAD) * CHUNK, CHUNK)
+            fetch(off, CHUNK, n % DEPTH).wait()
+        m = n // per
+        p_off = pl.multiple_of(m * WIDE, WIDE)
+
+        def arrive():
+            @pl.when(n % per == 0)
+            def _():
+                for k, p in enumerate(col_peers):
+                    p_send(p_off, WIDE, m, k, p).wait_recv()
+
+        ladder(off, CHUNK, n, vbuf.at[n % DEPTH], arrive)
+
+        @pl.when(n + DEPTH < n_full)
+        def _():
+            fetch(pl.multiple_of((n + DEPTH) * CHUNK, CHUNK), CHUNK, n % DEPTH).start()
+
+        @pl.when(jnp.logical_and(n % per == 0, m + P_AHEAD < n_wide))
+        def _():
+            later = pl.multiple_of((m + P_AHEAD) * WIDE, WIDE)
             for k, p in enumerate(col_peers):
-                p_send(later, CHUNK, n + P_AHEAD, k, p).start()
-
-        @pl.when(n + P_AHEAD == n_full)
+                p_send(later, WIDE, m + P_AHEAD, k, p).start()
+
+        @pl.when(n == (n_wide - P_AHEAD) * per)
         def _():
             for k, p in enumerate(col_peers):
-                p_send(n_full * CHUNK, LANES, n_full, k, p).start()
-
-        @pl.when(n == 2)
+                p_send(n_wide * WIDE, LANES, n_wide, k, p).start()
+
+        @pl.when(n == X_STEP)
         def _():
             with jax.named_scope("ph_form_x"):
                 form_x()
 
-        @pl.when(n == 6)
+        @pl.when(n == M_STEP)
         def _():
             with jax.named_scope("ph_form_m"):
                 form_m()
@@ -443,7 +458,12 @@
         def _():
             across(pl.multiple_of((n - 1) * CHUNK, CHUNK), CHUNK, n - 1)
 
-    ladder(n_full * CHUNK, LANES, n_full, vlast)
+    ld_last.wait()
+    def arrive_last():
+        for k, p in enumerate(col_peers):
+            p_send(n_wide * WIDE, LANES, n_wide, k, p).wait_recv()
+
+    ladder(n_full * CHUNK, LANES, n_full, vlast, arrive_last)
     across((n_full - 1) * CHUNK, CHUNK, n_full - 1)
     across(n_full * CHUNK, LANES, n_full)
 
@@ -487,44 +507,41 @@
             for k, p in enumerate(col_peers):
                 d_send(w, k, p).wait_recv()
 
-    own_d.wait()
-    wait_d(0)
-
-    @pl.loop(0, n_full)
-    def _(n):
-        @pl.when(n == n_cut)
-        def _():
-            wait_d(1)
-
-        with jax.named_scope("ph_fin_x"):
-            x_pass(full(n), CHUNK, n).wait_recv()
-        finish(full(n), CHUNK, n)
-
-    x_pass(n_full * CHUNK, LANES, n_full).wait_recv()
-    finish(n_full * CHUNK, tail, n_full)
-
     lad_p.wait_send()
     send_lo(0).wait_send()
-    for q in range(NQ):
-        send_y(q).wait_send()
-        send_z(q).wait_send()
-        send_dz(q).wait_send()
-        send_row(q).wait_send()
-        send_lx(q).wait_send()
     row_p.wait_send()
     row_o.wait_send()
+    own = rows.at[c]
+    for k in range(3):
+        remote(own, own, ts_sem.at[k], tr_sem.at[0, 0], r, c_y).wait_send()
+    remote(own, own, ls_sem.at[0], tr_sem.at[0, 0], r, c_y).wait_send()
+    remote(own, own, rx_sem.at[0], rx_sem.at[1], r_s, c).wait_send()
     for k, p in enumerate(row_peers):
         m_send(k, p).wait_send()
     for k, p in enumerate(col_peers):
         x_send(k, p).wait_send()
-        for w in range(2):
-            d_send(w, k, p).wait_send()
-    for n, (off, width) in enumerate(chunks):
-        for k, p in enumerate(col_peers):
-            p_send(off, width, n, k, p).wait_send()
-        for w in range(2):
-            h_send(off, width, n, w).wait_send()
-        x_pass(off, width, n).wait_send()
+        remote(msg_p.at[p], got_p.at[c], ps_sem.at[k], pr_sem.at[k, 0], r, p).wait_send()
+    for w in range(2):
+        remote(part.at[2 * w + 1 - u], half.at[w], hs_sem.at[w], hr_sem.at[w, 0], r_p, c).wait_send()
+
+    own_d.wait()
+    wait_d(0)
+
+    @pl.loop(0, n_full)
+    def _(n):
+        @pl.when(n == n_cut)
+        def _():
+            wait_d(1)
+
+        with jax.named_scope("ph_fin_x"):
+            x_pass(full(n), CHUNK, n).wait_recv()
+        finish(full(n), CHUNK, n)
+
+    x_pass(n_full * CHUNK, LANES, n_full).wait_recv()
+    finish(n_full * CHUNK, tail, n_full)
+    for k, p in enumerate(col_peers):
+        remote(msg_d.at[p], got_d.at[c], d_sem.at[0, k], d_sem.at[1, k], r, p).wait_send()
+    remote(part.at[r], half.at[0], xs_sem.at[0], xr_sem.at[0], r_s, c).wait_send()
 
 
 def solution(mesh):
@@ -552,8 +569,7 @@
         return pl.pallas_call(
             functools.partial(sweep_kernel, (n_occ, n_virt, n_row, n_col)),
             out_shape=pltpu.VMEM(block, F32),
-            grid=(1,),
-            in_specs=[hbm] * 4 + [pl.BlockSpec((cols_dev, LANES), lambda i: (0, cols_dev // LANES), pipeline_mode=pl.Buffered(1))] + [hbm] * 5,
+            in_specs=[hbm] * 9,
             out_specs=pl.BlockSpec(memory_space=pltpu.VMEM),
             scratch_shapes=[
                 vm(block, F32), vm((n_col,) + block, BF16), vm((n_row,) + block, BF16), vm((n_row,) + block, BF16),
@@ -564,17 +580,17 @@
                 vm((n_col, n_pair, wide), F32), vm((n_col, n_pair, wide), F32),
                 vm((n_row, rows_dev, wide), F32), vm((2, rows_dev, wide), F32),
                 vm((n_chunk, rows_dev, CHUNK), F32), vm((n_chunk, rows_dev, CHUNK), F32), vm((rows_dev, CHUNK), F32),
-                vm((2, cols_dev, CHUNK), BF16), vm(block, BF16), vm(oooo_full.shape, BF16),
+                vm((DEPTH, cols_dev, CHUNK), BF16), vm((cols_dev, cols_dev % CHUNK), BF16), vm(block, BF16), vm(oooo_full.shape, BF16),
                 vm((rows_dev, rows_dev), BF16), vm((n_sq, n_sq), BF16),
                 vm((rows_dev, n_sq), F32), vm((n_col, rows_dev, n_sq), F32),
                 vm((n_row, rows_dev, rows_dev), BF16), vm((n_row, rows_dev, rows_dev), BF16),
-                dma((10,)), dma((2,)), dma((2,)), dma((3, NQ)), dma((3, NQ)), dma((4, NQ)), dma((4, NQ)), dma((2, 4)),
-                dma((2, NQ)), dma((3, n_chunk)), dma((3, n_chunk)), dma((2, 2, 3)), dma((2, n_chunk)), dma((2, n_chunk)),
-                dma((n_chunk,)), dma((n_chunk,)), dma((2, 3)), dma((2, 3)),
+                dma((9,)), dma((DEPTH,)), dma((2,)), dma((3,)), dma((3, NQ)), dma((4,)), dma((2, NQ)), dma((2,)), dma((2, 4)),
+                dma((2,)), dma((3,)), dma((3, cols_dev // WIDE + 1)), dma((3, 3)), dma((2,)), dma((2, RING)),
+                dma((1,)), dma((n_chunk,)), dma((2, 3)), dma((2, 3)),
             ],
             compiler_params=pltpu.CompilerParams(
                 collective_id=0, has_side_effects=True, vmem_limit_bytes=65536000),
-        )(t_blk, d_blk, oovv_blk, vvvv_blk, vvvv_blk, oooo_full, wd_blk.T, wx_blk.T, jnp.asarray(perm), jnp.asarray(swap))
+        )(t_blk, d_blk, oovv_blk, vvvv_blk, oooo_full, wd_blk.T, wx_blk.T, jnp.asarray(perm), jnp.asarray(swap))
 
     return jax.shard_map(
         local_sweep, mesh=mesh,

time: 80.5 us -> 76.4 us (0.949)
  Pallas kernels: 79.1 us -> 75.2 us
    pallas_call x1, Pallas kernels: 79.1 us -> 75.2 us  [local_sweep(): pl.pallas_call(functools.partial(sweep_kernel, (n_occ, n_virt, n_row, n_c...]
where the time goes in v5:
time: 76.4 us; the launch traced here: 76.2 us
  Pallas kernels  75.2 us (98%)
  local copies, waits for them, and re-layouts  1.07 us (1%)
    pallas_call x1, Pallas kernels, local_sweep(): pl.pallas_call(functools.partial(sweep_kernel, (n_occ, n_virt, n_row, n_c...  75.2 us

profile of v5, /device:TPU:0, one launch (start us, length us, event | category | flops | bytes accessed | tf_op | source)
XLA Modules:
  0.0 76.2 jit_solution(10173289418229788543)
XLA Ops:
  0.0 75.2 %shard_map.91 = f32[64,5184]{1,0:T(8,128)S(1)} custom-call(f32[64,5184]{1,0:T(8,128)} %t_hbm.1, f32[64,5184]{1,0:T(8,128)} %den_hbm.1, bf16[64,5184]{1,0:T(8,128)(2,1)} %oovv_hbm.1, bf16[5184,5184]{1,0:T(8,128)(2,1)} %vvvv_hbm.1, bf16[256,256]{1,0:T(8,128)(2,1)} %oooo_hbm.1, bf16[576,2304]{1,0:T(8,128)(2,1)} %bitcast.2, bf16[576,2304]{1,0:T(8,128)(2,1)} %bitcast.3, ...), custom_call_target="tpu_custom_call" | custom-call | tf_op jit(solution)/shard_map/pallas_call | solution.py:569
  75.2 1.1 %copy.11 = f32[64,5184]{1,0:T(8,128)} copy(f32[64,5184]{1,0:T(8,128)S(1)} %shard_map.91) | data formatting | bytes 2654208

commit v6 on v5

--- a/solution.py
+++ b/solution.py
@@ -17,7 +17,7 @@
 RING = 4
 DEPTH = 4
 LANES = 128
-X_STEP, M_STEP = 6, 14
+ROW_STEP, X_STEP, M_STEP = 3, 6, 14
 D_FIRST, D_SECOND = 9, 13
 P_FIRST, P_AHEAD = 2, 6
 AHEAD = 2
@@ -58,7 +58,12 @@
     def load(src, dst, k):
         return pltpu.make_async_copy(src, dst, in_sem.at[k])
 
-    ld_t = load(t_hbm, t32, 0)
+    def ld_t(q):
+        at = pl.ds(q * qrows, qrows)
+        return load(t_hbm.at[at, :], t32.at[at, :], 9 + q)
+
+    for q in range(NQ):
+        ld_t(q).start()
     ld_wx = load(wx_hbm, wxt, 1)
     ld_wd = load(wd_hbm, wdt, 2)
     ld_oovv = load(oovv_hbm, oovv, 3)
@@ -66,17 +71,10 @@
     ld_perm = load(perm_hbm, perm, 5)
     ld_swap = load(swap_hbm, swap, 6)
     ld_den = load(den_hbm, t32, 7)
-    for ld in (ld_t, ld_wx, ld_wd, ld_oovv, ld_oooo, ld_perm, ld_swap):
-        ld.start()
 
     def fetch(off, width, slot):
         return pltpu.make_async_copy(vvvv_hbm.at[:, pl.ds(off, width)], vbuf.at[slot], vb_sem.at[slot])
 
-    for s in range(DEPTH):
-        fetch(s * CHUNK, CHUNK, s).start()
-
-    ld_last = load(vvvv_hbm.at[:, pl.ds(n_full * CHUNK, tail)], vlast, 8)
-    ld_last.start()
     barrier = pltpu.get_barrier_semaphore()
     for p in col_peers:
         pl.semaphore_signal(barrier, inc=1, device_id={"row": r, "col": p}, device_id_type=MESH)
@@ -122,8 +120,8 @@
     own_ladder = z == 1 - x
     direct = u == y
 
-    ld_t.wait()
     for q in range(NQ):
+        ld_t(q).wait()
         rows[c, pl.ds(q * qrows, qrows), :] = t32[pl.ds(q * qrows, qrows), :].astype(BF16)
         if q < AHEAD:
             send_y(q).start()
@@ -133,7 +131,14 @@
             def _():
                 send_lx(q).start()
 
+    for ld in (ld_wd, ld_wx, ld_swap, ld_perm, ld_oovv, ld_oooo):
+        ld.start()
     ld_den.start()
+    for s in range(DEPTH):
+        fetch(s * CHUNK, CHUNK, s).start()
+
+    ld_last = load(vvvv_hbm.at[:, pl.ds(n_full * CHUNK, tail)], vlast, 8)
+    ld_last.start()
 
     def send_row(q):
         return remote(piece(rows, c, q), piece(tcols, r, q), rx_sem.at[0], rx_sem.at[1], r_s, c)
@@ -247,7 +252,7 @@
             def _():
                 stage(q + 2)
 
-            on_step(q, 1, forward_ladder, 1)
+            on_step(q, 0, forward_ladder, 1)
             on_step(q, 1, go_row, 1)
             on_step(q, 2, forward_ladder, 3)
             on_step(q, 2, go_row, 2)
@@ -338,8 +343,6 @@
 
     own_p.wait()
 
-    remote(tcols.at[r_s], tcols.at[r_s], rx_sem.at[0], rx_sem.at[1], r_s, c).wait_recv()
-    row_o.start()
 
     def h_send(off, width, n, w):
         at = pl.ds(off, width)
@@ -430,6 +433,11 @@
         def _():
             for k, p in enumerate(col_peers):
                 p_send(n_wide * WIDE, LANES, n_wide, k, p).start()
+
+        @pl.when(n == ROW_STEP)
+        def _():
+            remote(tcols.at[r_s], tcols.at[r_s], rx_sem.at[0], rx_sem.at[1], r_s, c).wait_recv()
+            row_o.start()
 
         @pl.when(n == X_STEP)
         def _():
@@ -584,7 +592,7 @@
                 vm((rows_dev, rows_dev), BF16), vm((n_sq, n_sq), BF16),
                 vm((rows_dev, n_sq), F32), vm((n_col, rows_dev, n_sq), F32),
                 vm((n_row, rows_dev, rows_dev), BF16), vm((n_row, rows_dev, rows_dev), BF16),
-                dma((9,)), dma((DEPTH,)), dma((2,)), dma((3,)), dma((3, NQ)), dma((4,)), dma((2, NQ)), dma((2,)), dma((2, 4)),
+                dma((9 + NQ,)), dma((DEPTH,)), dma((2,)), dma((3,)), dma((3, NQ)), dma((4,)), dma((2, NQ)), dma((2,)), dma((2, 4)),
                 dma((2,)), dma((3,)), dma((3, cols_dev // WIDE + 1)), dma((3, 3)), dma((2,)), dma((2, RING)),
                 dma((1,)), dma((n_chunk,)), dma((2, 3)), dma((2, 3)),
             ],

time: 76.4 us -> 75.9 us (level)
  no operation moved by 1% of the time
where the time goes in v6:
time: 75.9 us; the launch traced here: 75.8 us
  Pallas kernels  74.7 us (98%)
  local copies, waits for them, and re-layouts  1.07 us (1%)
    pallas_call x1, Pallas kernels, local_sweep(): pl.pallas_call(functools.partial(sweep_kernel, (n_occ, n_virt, n_row, n_c...  74.7 us

profile of v6, /device:TPU:0, one launch (start us, length us, event | category | flops | bytes accessed | tf_op | source)
XLA Modules:
  0.0 75.8 jit_solution(16857774723017147829)
XLA Ops:
  0.0 74.7 %shard_map.91 = f32[64,5184]{1,0:T(8,128)S(1)} custom-call(f32[64,5184]{1,0:T(8,128)} %t_hbm.1, f32[64,5184]{1,0:T(8,128)} %den_hbm.1, bf16[64,5184]{1,0:T(8,128)(2,1)} %oovv_hbm.1, bf16[5184,5184]{1,0:T(8,128)(2,1)} %vvvv_hbm.1, bf16[256,256]{1,0:T(8,128)(2,1)} %oooo_hbm.1, bf16[576,2304]{1,0:T(8,128)(2,1)} %bitcast.2, bf16[576,2304]{1,0:T(8,128)(2,1)} %bitcast.3, ...), custom_call_target="tpu_custom_call" | custom-call | tf_op jit(solution)/shard_map/pallas_call | solution.py:577
  74.7 1.1 %copy.11 = f32[64,5184]{1,0:T(8,128)} copy(f32[64,5184]{1,0:T(8,128)S(1)} %shard_map.91) | data formatting | bytes 2654208

commit v7 on v6

--- a/solution.py
+++ b/solution.py
@@ -32,7 +32,7 @@
     t32, rows, lad, tcols, wd, wdt, wxt, tr, ta, r3, r5, sd, sp, msg_d, msg_p, got_d, got_p,
     part, half, xsend, xgot, turned, vbuf, vlast, oovv, oooo, perm, swap, xpart, xgot_part, m_mine, m_got,
     in_sem, vb_sem, loc_sem, ts_sem, tr_sem, ls_sem, lr_sem, ly_sem, g_sem,
-    rx_sem, ps_sem, pr_sem, d_sem, hs_sem, hr_sem, xs_sem, xr_sem, x_sem, m_sem,
+    rx_sem, ps_sem, pr_sem, ds_sem, d_sem, hs_sem, hr_sem, xs_sem, xr_sem, x_sem, m_sem,
 ):
     n_occ, n_virt, n_row, n_col = dims
     rows_dev, cols_dev = t32.shape
@@ -274,7 +274,7 @@
 
     def p_send(off, width, n, k, p):
         at = pl.ds(off, width)
-        return remote(msg_p.at[p, :, at], got_p.at[c, :, at], ps_sem.at[k], pr_sem.at[k, n], r, p)
+        return remote(msg_p.at[p, :, at], got_p.at[c, :, at], ps_sem.at[0], pr_sem.at[k, n], r, p)
 
     n_wide = cols_dev // WIDE
     chunks = [(n * WIDE, WIDE) for n in range(n_wide)] + [(n_wide * WIDE, LANES)]
@@ -292,7 +292,7 @@
 
     def d_send(w, k, p):
         at = pl.ds(*d_halves[w])
-        return remote(msg_d.at[p, :, at], got_d.at[c, :, at], d_sem.at[0, k], d_sem.at[1 + w, k], r, p)
+        return remote(msg_d.at[p, :, at], got_d.at[c, :, at], ds_sem.at[0], d_sem.at[w, k], r, p)
 
     own_d = pltpu.make_async_copy(msg_d.at[c], got_d.at[c], loc_sem.at[1])
 
@@ -373,7 +373,7 @@
             h_send(off, width, n, w).start()
 
     def x_send(k, p):
-        return remote(xpart, xgot_part.at[c], x_sem.at[0, k], x_sem.at[1, k], r, p)
+        return remote(xpart, xgot_part.at[c], x_sem.at[0], x_sem.at[1 + k], r, p)
 
     def form_x():
         row_p.wait_recv()
@@ -386,7 +386,7 @@
             x_send(k, p).start()
 
     def m_send(k, p):
-        return remote(m_mine.at[p], m_got.at[r], m_sem.at[0, k], m_sem.at[1, k], p, c)
+        return remote(m_mine.at[p], m_got.at[r], m_sem.at[0], m_sem.at[1 + k], p, c)
 
     def form_m():
         for k, p in enumerate(col_peers):
@@ -524,11 +524,10 @@
         remote(own, own, ts_sem.at[k], tr_sem.at[0, 0], r, c_y).wait_send()
     remote(own, own, ls_sem.at[0], tr_sem.at[0, 0], r, c_y).wait_send()
     remote(own, own, rx_sem.at[0], rx_sem.at[1], r_s, c).wait_send()
-    for k, p in enumerate(row_peers):
-        m_send(k, p).wait_send()
-    for k, p in enumerate(col_peers):
-        x_send(k, p).wait_send()
-        remote(msg_p.at[p], got_p.at[c], ps_sem.at[k], pr_sem.at[k, 0], r, p).wait_send()
+    three = pl.ds(0, 3)
+    remote(m_mine.at[three], m_got.at[three], m_sem.at[0], m_sem.at[1], r_p, c).wait_send()
+    remote(xgot_part.at[three], xgot_part.at[three], x_sem.at[0], x_sem.at[1], r, c_y).wait_send()
+    remote(msg_p.at[three], got_p.at[three], ps_sem.at[0], pr_sem.at[0, 0], r, c_y).wait_send()
     for w in range(2):
         remote(part.at[2 * w + 1 - u], half.at[w], hs_sem.at[w], hr_sem.at[w, 0], r_p, c).wait_send()
 
@@ -547,8 +546,7 @@
 
     x_pass(n_full * CHUNK, LANES, n_full).wait_recv()
     finish(n_full * CHUNK, tail, n_full)
-    for k, p in enumerate(col_peers):
-        remote(msg_d.at[p], got_d.at[c], d_sem.at[0, k], d_sem.at[1, k], r, p).wait_send()
+    remote(msg_d.at[three], got_d.at[three], ds_sem.at[0], d_sem.at[0, 0], r, c_y).wait_send()
     remote(part.at[r], half.at[0], xs_sem.at[0], xr_sem.at[0], r_s, c).wait_send()
 
 
@@ -593,8 +591,8 @@
                 vm((rows_dev, n_sq), F32), vm((n_col, rows_dev, n_sq), F32),
                 vm((n_row, rows_dev, rows_dev), BF16), vm((n_row, rows_dev, rows_dev), BF16),
                 dma((9 + NQ,)), dma((DEPTH,)), dma((2,)), dma((3,)), dma((3, NQ)), dma((4,)), dma((2, NQ)), dma((2,)), dma((2, 4)),
-                dma((2,)), dma((3,)), dma((3, cols_dev // WIDE + 1)), dma((3, 3)), dma((2,)), dma((2, RING)),
-                dma((1,)), dma((n_chunk,)), dma((2, 3)), dma((2, 3)),
+                dma((2,)), dma((1,)), dma((3, cols_dev // WIDE + 1)), dma((1,)), dma((2, 3)), dma((2,)), dma((2, RING)),
+                dma((1,)), dma((n_chunk,)), dma((4,)), dma((4,)),
             ],
             compiler_params=pltpu.CompilerParams(
                 collective_id=0, has_side_effects=True, vmem_limit_bytes=65536000),

time: 75.9 us -> 75.8 us (level)
  no operation moved by 1% of the time
where the time goes in v7:
time: 75.8 us; the launch traced here: 75.7 us
  Pallas kernels  74.6 us (98%)
  local copies, waits for them, and re-layouts  1.07 us (1%)
    pallas_call x1, Pallas kernels, local_sweep(): pl.pallas_call(functools.partial(sweep_kernel, (n_occ, n_virt, n_row, n_c...  74.6 us

profile of v7, /device:TPU:0, one launch (start us, length us, event | category | flops | bytes accessed | tf_op | source)
XLA Modules:
  0.0 75.7 jit_solution(882901646918963536)
XLA Ops:
  0.0 74.6 %shard_map.91 = f32[64,5184]{1,0:T(8,128)S(1)} custom-call(f32[64,5184]{1,0:T(8,128)} %t_hbm.1, f32[64,5184]{1,0:T(8,128)} %den_hbm.1, bf16[64,5184]{1,0:T(8,128)(2,1)} %oovv_hbm.1, bf16[5184,5184]{1,0:T(8,128)(2,1)} %vvvv_hbm.1, bf16[256,256]{1,0:T(8,128)(2,1)} %oooo_hbm.1, bf16[576,2304]{1,0:T(8,128)(2,1)} %bitcast.2, bf16[576,2304]{1,0:T(8,128)(2,1)} %bitcast.3, ...), custom_call_target="tpu_custom_call" | custom-call | tf_op jit(solution)/shard_map/pallas_call | solution.py:575
  74.6 1.1 %copy.11 = f32[64,5184]{1,0:T(8,128)} copy(f32[64,5184]{1,0:T(8,128)S(1)} %shard_map.91) | data formatting | bytes 2654208
